TPU v7x, 256 devices: a whole 4x4x8 slice. The times are simulated.
256 devices in a mesh: row: 16 (over y, x), col: 16 (over z, core).
Axes of the slice: x: 4, y: 4, z: 8, core: 2. Of those that a mesh axis runs over, the one named last changes fastest.
Arguments:
- tile_data: bfloat16 [1024, 128, 128], P(('row', 'col')), may hold values from -24 to 24
- tile_coords: int32 [3, 1024], P(None, ('row', 'col')), may hold values from 0 to 2047, as said below
- tile_counts: int32 [256], P(('row', 'col')), may hold values from 1 to 4, as said below
- factor_rows: float32 [64, 32768], P(None, ('row', 'col')), may hold values from -6 to 6
- factor_cols: float32 [64, 32768], P(None, ('col', 'row')), may hold values from -6 to 6
- factor_depth: float32 [64, 2048], P(None, ('row', 'col')), may hold values from -6 to 6
- damping: float32 [], replicated, may hold values from 128 to 512
Outputs:
- step_a: float32 [64, 32768], P(None, ('row', 'col'))
- step_b: float32 [64, 32768], P(None, ('col', 'row'))
- step_c: float32 [64, 2048], P(None, ('row', 'col'))
Inputs may be any that keep to these rules, and one draw needn't show every extreme that they name: `tile_coords`: the first row names a tile's block within its device's group of 16 first-mode blocks, the second its block within the group of 16 second-mode blocks, the third its third-mode index below 2048. `tile_counts`: slots at and beyond a device's count are padding and carry nothing; some device fills all 4 slots.
All inputs are finite; a program needn't handle non-finite values.
Results may differ from a plain program's by a relative error of at most 0.0003.
Values sent between devices are 32-bit elements; how exact they have to be, the bound alone decides.
No kernel may reach another device: no remote copies, remote signals or barrier semaphores. Data moves between devices by JAX's collectives and lax.ppermute only.
A program may use at most 64 MiB of HBM per device.

v0:
```python
import functools

import jax
import jax.numpy as jnp
from jax import lax
from jax.experimental import pallas as pl
from jax.experimental.pallas import tpu as pltpu
from jax.sharding import Mesh
from jax.sharding import PartitionSpec as P


ROW = ("y", "x")
ALL = ("y", "x", "z", "c")
ROW_COL = ("y", "x", "z", "c")
COL_ROW = ("z", "c", "y", "x")
R = 64
T = 128
TILES = 4
NZ = 8
NP = 16
F32 = jnp.float32

VMEM = pl.BlockSpec(memory_space=pltpu.VMEM)
SMEM = pl.BlockSpec(memory_space=pltpu.SMEM)


def halves(a):
    high = a.astype(jnp.bfloat16)
    return high, (a - high.astype(F32)).astype(jnp.bfloat16)


def pass_of(a, b, ca, cb):
    return lax.dot_general(a, b, (((ca,), (cb,)), ((), ())), preferred_element_type=F32)


def dot(a, b, ca, cb):
    (a_high, a_low), (b_high, b_low) = halves(a), halves(b)
    small = pass_of(a_low, b_high, ca, cb) + pass_of(a_high, b_low, ca, cb)
    return small + pass_of(a_high, b_high, ca, cb)


def shaped(*shape):
    return jax.ShapeDtypeStruct(shape, F32)


def call(body, outs, ins, scalars=0, limit=16):
    return pl.pallas_call(
        body,
        out_shape=outs,
        in_specs=[SMEM] * scalars + [VMEM] * (len(ins) - scalars),
        out_specs=jax.tree.map(lambda _: VMEM, outs),
        compiler_params=pltpu.CompilerParams(vmem_limit_bytes=limit * 2**20),
    )(*ins)


def lanes(shape):
    return lax.broadcasted_iota(jnp.int32, shape, len(shape) - 1)


def rows_of(shape):
    return lax.broadcasted_iota(jnp.int32, shape, len(shape) - 2)


def decode(code):
    return code % 2, (code // 2) % 8, (code // 16) % 4, (code // 64) % 4


def start_body(fr, fd, fc, out, near):
    near[...] = fc[...]
    columns = jnp.concatenate([fd[...], jnp.zeros((8, T - R), F32)], axis=1)
    a = fr[...]
    for z in range(NZ):
        out[z, :R] = a
        out[z, R : R + 8] = columns


def turn_body(gz, b0, b1, b2, b3, out, stack):
    for k, part in enumerate((b0, b1, b2, b3)):
        stack[k] = part[...]
    low = jnp.concatenate([gz[z, R : R + 8] for z in range(4)], axis=0)
    high = jnp.concatenate([gz[z, R : R + 8] for z in range(4, 8)], axis=0)
    packed = jnp.where(lanes((32, T)) < R, low, pltpu.roll(high, R, 1))
    for p in range(NP):
        out[p] = packed


def back(index, code):
    _, _, x, y = decode(code)
    return jnp.bitwise_xor(y, index // 4), jnp.bitwise_xor(x, index % 4)


def pair_place(there, here):
    return jnp.bitwise_xor(there, here)


def scatter_tile(t, coords, code, grad_a, grad_b, keep, send, fb):
    core, z_here, _, _ = decode(code)
    block = jnp.bitwise_and(coords[0, t], NP - 1)
    mine = jnp.bitwise_xor(block % 2, core) == 0
    place = pair_place(block // 2, z_here)
    keep[place] += jnp.where(mine, grad_a, 0.0)
    send[place] += jnp.where(mine, 0.0, grad_a)
    fb[jnp.bitwise_and(coords[1, t], NP - 1)] += grad_b


def pick_a(t, coords, code, own, oth):
    block = jnp.bitwise_and(coords[0, t], NP - 1)
    place, other = block // 2, jnp.bitwise_xor(block % 2, code % 2)
    return jnp.where(other == 0, own[place, :R], oth[place, :R])


def pick_pair(t, coords, code, own, oth):
    core, z_here, _, _ = decode(code)
    block = jnp.bitwise_and(coords[0, t], NP - 1)
    place = pair_place(block // 2, z_here)
    return jnp.where(jnp.bitwise_xor(block % 2, core) == 0, own[place], oth[place])


def pick_b(t, coords, code, stacks):
    down, along = back(jnp.bitwise_and(coords[1, t], NP - 1), code)
    found = stacks[0][along, :R]
    for m in range(1, 4):
        found = jnp.where(down == m, stacks[m][along, :R], found)
    return found


def depth_rows(products):
    sums = dot(jnp.ones((8, T), F32), jnp.concatenate(products, axis=0), 1, 1)
    return jnp.concatenate([sums[:1, :T], sums[:1, T:], jnp.zeros((6, T), F32)], axis=0)


def send_back(coords, code, values, rows_a, rows_b, rows_c, keep, send, fb):
    raws = [dot(b, v, 1, 1) for v, b in zip(values, rows_b)]
    grads_b = [dot(a * c, v, 1, 0) for v, a, c in zip(values, rows_a, rows_c)]
    depth = depth_rows([a * raw for a, raw in zip(rows_a, raws)])
    keep[...] = jnp.zeros(keep.shape, F32)
    send[...] = jnp.zeros(send.shape, F32)
    fb[...] = jnp.zeros(fb.shape, F32)
    for t in range(TILES):
        scatter_tile(t, coords, code, raws[t] * rows_c[t], grads_b[t], keep, send, fb)
    return depth


def first_body(
    coords, counts, code_ref, gz, oz, b0, b1, b2, b3, gr, orr, data,
    keep, send, fb, ta, tb, tc,
):
    code = code_ref[0]
    core = code % 2
    picked = []
    lane_row = lanes((1, T))
    for t in range(TILES):
        k = jnp.bitwise_and(coords[2, t], 2047)
        far, near = k // T, k % T
        q, j = near // 8, near % 8
        z = q // 2
        place = (z % 4) * 8 + j
        own = gr[far, pl.ds(place, 1), :]
        oth = orr[far, pl.ds(place, 1), :]
        row = jnp.where(jnp.bitwise_xor(q % 2, core) == 0, own, oth)
        row = jnp.where(z // 4 == 0, row, pltpu.roll(row, R, 1))
        picked.append(jnp.where(lane_row < R, row, 0.0))
    chosen = jnp.concatenate([*picked, jnp.zeros((T - TILES, T), F32)], axis=0)
    column = chosen.T[:R]
    tc[...] = column
    rows_a = [pick_a(t, coords, code, gz, oz) for t in range(TILES)]
    rows_b = [pick_b(t, coords, code, (b0, b1, b2, b3)) for t in range(TILES)]
    rows_c = [column[:, t : t + 1] for t in range(TILES)]
    models = [dot(a, b * c, 0, 0) for a, b, c in zip(rows_a, rows_b, rows_c)]
    values = [
        jnp.where(t < counts[0], data[t].astype(F32) - models[t], 0.0) for t in range(TILES)
    ]
    for t in range(TILES):
        ta[t] = rows_a[t]
        tb[t] = rows_b[t]
    rows = send_back(coords, code, values, rows_a, rows_b, rows_c, keep, send, fb)
    row, lane = rows_of((8, T)), lanes((8, T))
    for t in range(TILES):
        rows = jnp.where((row == 2) & (lane == t), coords[2, t].astype(F32), rows)
    send[NZ, :8] = rows


def join_body(keep, send, received, out):
    mine, theirs = send[NZ, :8], received[NZ, :8]
    extra = jnp.where(lanes((1, T)) < 4, mine[2:3], pltpu.roll(theirs, 4, 1)[2:3])
    pad = jnp.zeros((2, T), F32)
    rows = jnp.concatenate([mine[:2], theirs[:2], extra, mine[2:3] + theirs[2:3], pad], axis=0)
    for k in range(4):
        out[k, :R] = keep[2 * k] + received[2 * k]
        out[k, R : 2 * R] = keep[2 * k + 1] + received[2 * k + 1]
        out[k, 2 * R :] = rows


def pair_body(s0, s1, s2, s3, out):
    out[: 2 * R] = s0[0, : 2 * R] + s1[: 2 * R] + s2[: 2 * R] + s3[: 2 * R]
    for k, part in enumerate((s0[0, 2 * R :], s1[2 * R :], s2[2 * R :], s3[2 * R :])):
        out[2 * R + 8 * k : 2 * R + 8 * k + 8] = part


def sum_body(mine, received, gr, ga, gb, couple, out, *, scalars):
    own = mine[:R] + received[R : 2 * R]
    ga[...] = own
    couple[0] = own
    couple[1] = mine[R : 2 * R] + received[:R]
    total = gr[0]
    for p in range(1, NP):
        total = total + gr[p]
    gb[...] = total
    blocks = [half[2 * R + 8 * k : 2 * R + 8 * k + 8] for half in (mine, received) for k in range(4)]
    rows = jnp.concatenate([b[g : g + 1] for g in range(4) for b in blocks], axis=0)
    extra = jnp.concatenate([b[4:5] for b in blocks], axis=0)
    if scalars:
        extra = blocks[0]
        for b in blocks[1:]:
            extra = extra + b
    for p in range(NP):
        out[p, :R] = total
        out[p, R : R + 32] = rows
        out[p, R + 32 : R + 40] = extra


def line_body(s0, s1, s2, s3, out):
    for k, part in enumerate((s0, s1, s2, s3)):
        out[2 * k : 2 * k + 2] = part[...]


def depth_sums(coords, code, br, index):
    lane = lanes((1, T))
    near = jnp.bitwise_and(lane, 15)
    wanted = jnp.where(near >= 8, (code * 8 + near - 8).astype(F32), -1.0)
    for t in range(TILES):
        wanted = jnp.where(near == t, coords[2, t].astype(F32), wanted)
    rows = br[:, R : R + 32, :].reshape(NP * 32, T)
    known = jnp.where(lanes((NP * 32, T)) < 16, index[:, :1], index[:, 1:2])
    chosen = (known == wanted).astype(F32).astype(jnp.bfloat16)
    high, low = halves(rows)
    part = pass_of(low, chosen, 0, 0) + pass_of(high, chosen, 0, 0)
    return part[:R] + pltpu.roll(part[R:], T - 16, 1)


def apply_tile(t, coords, code, az, ao, br, ta, tb, tc, sums):
    a, b, c = ta[t], tb[t], tc[:, t : t + 1]
    da = pick_pair(t, coords, code, az, ao)
    db = br[jnp.bitwise_and(coords[1, t], NP - 1), :R]
    dc = sums[:, t : t + 1]
    left = jnp.concatenate([da, a], axis=0)
    right = jnp.concatenate([b * c, db * c + b * dc], axis=0)
    return dot(left, right, 0, 0), a, b, c


def owned(sums):
    lane = lanes((R, T))
    return jnp.where((lane >= 8) & (lane < 16), sums, 0.0)


def middle_body(
    coords, counts, code_ref, az, ao, br, ta, tb, tc, ga, gb,
    keep, send, fb, w, gc, index,
):
    code = code_ref[0]
    lane = lanes((8, T))
    for p in range(NP):
        known = br[p, R + 32 : R + 40]
        for g in range(4):
            low, high = known[:, 2 * g : 2 * g + 1], known[:, 2 * g + 1 : 2 * g + 2]
            index[32 * p + 8 * g : 32 * p + 8 * g + 8] = jnp.where(lane == 0, low, high)
    sums = depth_sums(coords, code, br, index)
    mine = owned(sums)
    gc[...] = mine
    norm = jnp.sum(ga[...] * ga[...] + gb[...] * gb[...] + mine * mine)
    made = [apply_tile(t, coords, code, az, ao, br, ta, tb, tc, sums) for t in range(TILES)]
    values = [jnp.where(t < counts[0], made[t][0], 0.0) for t in range(TILES)]
    rows_a, rows_b, rows_c = ([m[i] for m in made] for i in (1, 2, 3))
    curve = jnp.zeros((T, T), F32)
    for t in range(TILES):
        w[t] = values[t]
        curve = curve + values[t] * values[t]
    out = send_back(coords, code, values, rows_a, rows_b, rows_c, keep, send, fb)
    row, lane = rows_of((8, T)), lanes((8, T))
    out = jnp.where((row == 2) & (lane == 0), norm, out)
    send[NZ, :8] = jnp.where((row == 2) & (lane == 1), jnp.sum(curve), out)


def both_norms(br):
    total = jnp.sum(br[:, R + 32 : R + 40, :], axis=0)
    row, lane = rows_of((8, T)), lanes((8, T))
    norm = jnp.sum(jnp.where((row == 5) & (lane == 0), total, 0.0))
    curve = jnp.sum(jnp.where((row == 5) & (lane == 1), total, 0.0))
    return norm, curve


def last_body(
    coords, counts, code_ref, az, ao, br, index, ta, tb, tc, w,
    ga0, gb0, gc0, ga1, gb1, ha, hb, hc, out, spread,
):
    code = code_ref[0]
    norm, curve = both_norms(br)
    mu = jnp.full((1, 1), curve, F32) / jnp.full((1, 1), norm, F32)
    sums = depth_sums(coords, code, br, index)
    a_rest = ga1[...] - mu * ga0[...]
    b_rest = gb1[...] - mu * gb0[...]
    c_rest = owned(sums) - mu * gc0[...]
    ha[...] = a_rest
    hb[...] = b_rest
    hc[...] = c_rest
    rest = jnp.sum(a_rest * a_rest + b_rest * b_rest + c_rest * c_rest)
    bend = jnp.zeros((T, T), F32)
    for t in range(TILES):
        product, _, _, _ = apply_tile(t, coords, code, az, ao, br, ta, tb, tc, sums)
        v = jnp.where(t < counts[0], product, 0.0) - mu * w[t]
        bend = bend + v * v
    row, lane = rows_of((8, T)), lanes((8, T))
    put = jnp.where((row == 0) & (lane == 0), rest, 0.0)
    put = jnp.where((row == 0) & (lane == 1), jnp.sum(bend), put)
    put = jnp.where((row == 0) & (lane == 2), norm, put)
    put = jnp.where((row == 0) & (lane == 3), curve, put)
    out[...] = put
    spread[...] = jnp.broadcast_to(put[:1][None], spread.shape)


def end_body(damping, sums, own, ga0, gb0, gc0, ha, hb, hc, oa, ob, oc):
    lane = lanes((1, T))

    def scalar(ref, at):
        return jnp.sum(jnp.where(lane == at, ref[:1], 0.0), axis=1, keepdims=True)

    rest, bend = scalar(sums, 0), scalar(sums, 1)
    norm, curve = scalar(own, 2), scalar(own, 3)
    lam = damping[0]
    mu = curve / norm
    nu = 1.0 / (mu + lam)
    ratio = rest / norm
    second = 1.0 / (bend / rest + lam - ratio * nu)
    on_g = nu + second * ratio * nu * nu
    on_h = -second * nu
    oa[...] = on_g * ga0[...] + on_h * ha[...]
    ob[...] = on_g * gb0[...] + on_h * hb[...]
    oc[...] = (on_g * gc0[...] + on_h * hc[...]).T[8:16]


def along_z(x):
    return lax.all_to_all(x, "z", 0, 0, tiled=True)


def along_row(x):
    return lax.all_to_all(x, ROW, 0, 0, tiled=True)


def swap(x):
    return lax.ppermute(x, "c", [(0, 1), (1, 0)])


def shift(x, axis, k):
    return lax.ppermute(x, axis, [(i, i ^ k) for i in range(4)])


def from_near(x, axis):
    return tuple(shift(x, axis, k) for k in range(1, 4))


def pair_shift(x, k):
    return lax.ppermute(x, "z", [(i, i ^ (2 * k)) for i in range(8)])


def pair_swap(x):
    return lax.ppermute(x, "z", [(i, i ^ 1) for i in range(8)])


def shares(keep, send, fb, scalars):
    joined = call(join_body, shaped(4, 2 * R + 8, T), (keep, send, swap(send)))
    gr = along_row(fb)
    strides = tuple(pair_shift(joined[k], k) for k in range(1, 4))
    mine = call(
        pair_body,
        shaped(2 * R + 32, T),
        (joined, *strides),
    )
    ga, gb, couple, payload = call(
        functools.partial(sum_body, scalars=scalars),
        (shaped(R, T), shaped(R, T), shaped(2, R, T), shaped(NP, R + 40, T)),
        (mine, pair_swap(mine), gr),
    )
    br = along_row(payload)
    line = [couple]
    for k in range(1, 4):
        line.append(pair_shift(couple, k))
    az = call(line_body, shaped(NZ, R, T), line)
    return ga, gb, (az, swap(az), br)


def step_of(data, coords, counts, fr, fc, fd, damping):
    code = lax.axis_index(ROW_COL).reshape(1)
    first, fc = call(
        start_body, (shaped(NZ, R + 8, T), shaped(R, T)), (fr, fd.T, fc), limit=60
    )
    gz = along_z(first)
    payload, stack = call(
        turn_body, (shaped(NP, 32, T), shaped(4, R, T)), (gz, fc, *from_near(fc, "x"))
    )
    gr = along_row(payload)
    gr, *stacks = lax.optimization_barrier((gr, stack, *from_near(stack, "y")))
    folded = (shaped(NZ, R, T), shaped(NZ + 1, R, T), shaped(NP, R, T))
    saved = (shaped(TILES, R, T), shaped(TILES, R, T), shaped(R, T))
    keep, send, fb, ta, tb, tc = call(
        first_body,
        folded + saved,
        (coords, counts, code, gz, swap(gz), *stacks, gr, swap(gr), data),
        3,
    )
    ga0, gb0, gathered = shares(keep, send, fb, False)
    keep, send, fb, w, gc0, index = call(
        middle_body,
        folded + (shaped(TILES, T, T), shaped(R, T), shaped(NP * 32, T)),
        (coords, counts, code, *gathered, ta, tb, tc, ga0, gb0),
        3,
    )
    ga1, gb1, gathered = shares(keep, send, fb, True)
    ha, hb, hc, own, spread = call(
        last_body,
        (shaped(R, T), shaped(R, T), shaped(R, T), shaped(8, T), shaped(256, 1, T)),
        (coords, counts, code, *gathered, index, ta, tb, tc, w, ga0, gb0, gc0, ga1, gb1),
        3,
    )
    sums = jnp.sum(lax.all_to_all(spread, ALL, 0, 0, tiled=True), axis=0)
    step_a, step_b, step_c = call(
        end_body,
        (shaped(R, T), shaped(R, T), shaped(8, R)),
        (damping.reshape(1), sums, own, ga0, gb0, gc0, ha, hb, hc),
        1,
    )
    return step_a, step_b, step_c.T


def solution(mesh):
    finer = Mesh(mesh.devices.reshape(4, 4, 8, 2), ("y", "x", "z", "c"))
    in_specs = (
        P(ROW_COL, None, None),
        P(None, ROW_COL),
        P(ROW_COL),
        P(None, ROW_COL),
        P(None, COL_ROW),
        P(None, ROW_COL),
        P(),
    )
    out_specs = (P(None, ROW_COL), P(None, COL_ROW), P(None, ROW_COL))
    return jax.shard_map(
        step_of, mesh=finer, in_specs=in_specs, out_specs=out_specs, check_vma=False
    )
```

profile of v0, /device:TPU:1, one launch (start us, length us, event | category | flops | bytes accessed | tf_op | source)
XLA Modules:
  0.0 165.7 jit_solution(2238928730570318652)
XLA Ops:
  0.6 1.5 shard_map.94
  2.2 9.1 %all-to-all-start = ((f32[8,72,128]{2,1,0:T(8,128)}), f32[8,72,128]{2,1,0:T(8,128)S(1)}, u32[]{:S(2)}, u32[]{:S(2)}) async-start(f32[8,72,128]{2,1,0:T(8,128)} %get-tuple-element.40), calls=%async_computation | async-start | bytes 589824 | tf_op jit(solution)/shard_map/all_to_all | solution.py:342
  11.3 1.3 collective-permute-start.1
  12.6 2.5 %collective-permute-start.2 = (f32[64,128]{1,0:T(8,128)S(1)}, f32[64,128]{1,0:T(8,128)S(1)}, u32[]{:S(2)}, u32[]{:S(2)}) collective-permute-start(f32[64,128]{1,0:T(8,128)S(1)} %copy-done.1), channel_id=1, source_target_pairs={{0,32},{16,48},{32,0},{48,16},{1,33},{17,49},{33,1},{49,17},{2,34}... | collective-permute-start | bytes 98312 | tf_op jit(solution)/shard_map/ppermute | solution.py:354
  15.2 1.6 collective-permute-done.2.b2
  16.9 2.5 %collective-permute-done.3.b3 = f32[64,128]{1,0:T(8,128)S(1)} collective-permute-done((f32[64,128]{1,0:T(8,128)S(1)}, f32[64,128]{1,0:T(8,128)S(1)}, u32[]{:S(2)}, u32[]{:S(2)}) %collective-permute-start.3) | collective-permute-done | bytes 32800 | tf_op jit(solution)/shard_map/ppermute | solution.py:354
  19.3 3.2 %all-to-all-done.gz = f32[8,72,128]{2,1,0:T(8,128)S(1)} async-done(((f32[8,72,128]{2,1,0:T(8,128)}), f32[8,72,128]{2,1,0:T(8,128)S(1)}, u32[]{:S(2)}, u32[]{:S(2)}) %all-to-all-start) | async-done | bytes 294944 | tf_op jit(solution)/shard_map/all_to_all | solution.py:342
  23.4 6.9 %all-to-all-start.1 = ((f32[16,32,128]{2,1,0:T(8,128)}), f32[16,32,128]{2,1,0:T(8,128)S(1)}, u32[]{:S(2)}, u32[]{:S(2)}) async-start(f32[16,32,128]{2,1,0:T(8,128)} %get-tuple-element.42), calls=%async_computation.1 | async-start | bytes 524288 | tf_op jit(solution)/shard_map/all_to_all | solution.py:346
  30.2 1.4 collective-permute-start.4
  31.6 2.4 %collective-permute-start.5 = (f32[4,64,128]{2,1,0:T(8,128)S(1)}, f32[4,64,128]{2,1,0:T(8,128)S(1)}, u32[]{:S(2)}, u32[]{:S(2)}) collective-permute-start(f32[4,64,128]{2,1,0:T(8,128)S(1)} %get-tuple-element.44.b0), channel_id=1, source_target_pairs={{0,128},{64,192},{128,0},{192,64},{1,129},{65,193},{129,1},{193,65... | collective-permute-start | bytes 393224 | tf_op jit(solution)/shard_map/ppermute | solution.py:354
  34.2 3.4 %collective-permute-start = (f32[8,72,128]{2,1,0:T(8,128)S(1)}, f32[8,72,128]{2,1,0:T(8,128)S(1)}, u32[]{:S(2)}, u32[]{:S(2)}) collective-permute-start(f32[8,72,128]{2,1,0:T(8,128)S(1)} %all-to-all-done.gz), channel_id=1, source_target_pairs={{0,1},{1,0},{2,3},{3,2},{4,5},{5,4},{6,7},{7,6},{8,9},{9,8},{10,11... | collective-permute-start | bytes 884744 | tf_op jit(solution)/shard_map/ppermute | solution.py:350
  37.6 3.5 %collective-permute-done.5.b2 = f32[4,64,128]{2,1,0:T(8,128)S(1)} collective-permute-done((f32[4,64,128]{2,1,0:T(8,128)S(1)}, f32[4,64,128]{2,1,0:T(8,128)S(1)}, u32[]{:S(2)}, u32[]{:S(2)}) %collective-permute-start.5) | collective-permute-done | bytes 131104 | tf_op jit(solution)/shard_map/ppermute | solution.py:354
  41.1 2.3 %collective-permute-done.6.b3 = f32[4,64,128]{2,1,0:T(8,128)S(1)} collective-permute-done((f32[4,64,128]{2,1,0:T(8,128)S(1)}, f32[4,64,128]{2,1,0:T(8,128)S(1)}, u32[]{:S(2)}, u32[]{:S(2)}) %collective-permute-start.6) | collective-permute-done | bytes 131104 | tf_op jit(solution)/shard_map/ppermute | solution.py:354
  43.4 1.7 %collective-permute-start.7 = (f32[16,32,128]{2,1,0:T(8,128)S(1)}, f32[16,32,128]{2,1,0:T(8,128)S(1)}, u32[]{:S(2)}, u32[]{:S(2)}) collective-permute-start(f32[16,32,128]{2,1,0:T(8,128)S(1)} %all-to-all-done.1.gr), channel_id=1, source_target_pairs={{0,1},{1,0},{2,3},{3,2},{4,5},{5,4},{6,7},{7,6},{8,9},{9,8},{10,11... | collective-permute-start | bytes 786440 | tf_op jit(solution)/shard_map/ppermute | solution.py:350
  46.5 2.4 %shard_map.96 = (f32[8,64,128]{2,1,0:T(8,128)S(1)}, f32[9,64,128]{2,1,0:T(8,128)S(1)}, f32[16,64,128]{2,1,0:T(8,128)}, f32[4,64,128]{2,1,0:T(8,128)S(1)}, f32[4,...) custom-call(s32[3,4]{1,0:T(4,128)S(1)} %copy-done.2, s32[1]{0:T(128)S(6)} %copy.10.counts, s32[1]{0:T(128)} %bitcast.1.code_ref, ...), custom_call_target="tpu_custom_call" | custom-call | tf_op jit(solution)/shard_map/pallas_call | solution.py:47
  49.0 3.9 %all-to-all-start.2 = ((f32[16,64,128]{2,1,0:T(8,128)}), f32[16,64,128]{2,1,0:T(8,128)S(1)}, u32[]{:S(2)}, u32[]{:S(2)}) async-start(f32[16,64,128]{2,1,0:T(8,128)} %get-tuple-element.51), calls=%async_computation.2 | async-start | bytes 1048576 | tf_op jit(solution)/shard_map/all_to_all | solution.py:346
  53.1 1.2 collective-permute-start.10
  54.3 1.6 collective-permute-start.11
  56.0 2.9 %collective-permute-start.9 = (f32[136,128]{1,0:T(8,128)S(1)}, f32[136,128]{1,0:T(8,128)S(1)}, u32[]{:S(2)}, u32[]{:S(2)}) collective-permute-start(f32[136,128]{1,0:T(8,128)S(1)} %get-tuple-element.82), channel_id=1, source_target_pairs={{0,4},{2,6},{4,0},{6,2},{8,12},{10,14},{12,8},{14,10},{1,5},{3,7},... | collective-permute-start | bytes 208904 | tf_op jit(solution)/shard_map/ppermute | solution.py:362
  58.8 1.6 collective-permute-done.10.s2
  60.9 3.2 %collective-permute-start.12 = (f32[160,128]{1,0:T(8,128)S(1)}, f32[160,128]{1,0:T(8,128)S(1)}, u32[]{:S(2)}, u32[]{:S(2)}) collective-permute-start(f32[160,128]{1,0:T(8,128)S(1)} %shard_map.98.mine), channel_id=1, source_target_pairs={{0,2},{2,0},{4,6},{6,4},{8,10},{10,8},{12,14},{14,12},{1,3},{3,1},... | collective-permute-start | bytes 245768 | tf_op jit(solution)/shard_map/ppermute | solution.py:366
  64.1 1.8 %collective-permute-done.12.received = f32[160,128]{1,0:T(8,128)S(1)} collective-permute-done((f32[160,128]{1,0:T(8,128)S(1)}, f32[160,128]{1,0:T(8,128)S(1)}, u32[]{:S(2)}, u32[]{:S(2)}) %collective-permute-start.12) | collective-permute-done | bytes 81952 | tf_op jit(solution)/shard_map/ppermute | solution.py:366
  66.9 5.8 %all-to-all-start.3 = ((f32[16,104,128]{2,1,0:T(8,128)}), f32[16,104,128]{2,1,0:T(8,128)S(1)}, u32[]{:S(2)}, u32[]{:S(2)}) async-start(f32[16,104,128]{2,1,0:T(8,128)} %get-tuple-element.53), calls=%async_computation.3 | async-start | bytes 1703936 | tf_op jit(solution)/shard_map/all_to_all | solution.py:346
  72.8 3.7 %collective-permute-start.13 = (f32[2,64,128]{2,1,0:T(8,128)S(1)}, f32[2,64,128]{2,1,0:T(8,128)S(1)}, u32[]{:S(2)}, u32[]{:S(2)}) collective-permute-start(f32[2,64,128]{2,1,0:T(8,128)S(1)} %get-tuple-element.52.s0), channel_id=1, source_target_pairs={{0,4},{2,6},{4,0},{6,2},{8,12},{10,14},{12,8},{14,10},{1,5},{3,7},... | collective-permute-start | bytes 196616 | tf_op jit(solution)/shard_map/ppermute | solution.py:362
  76.5 1.7 %collective-permute-start.14 = (f32[2,64,128]{2,1,0:T(8,128)S(1)}, f32[2,64,128]{2,1,0:T(8,128)S(1)}, u32[]{:S(2)}, u32[]{:S(2)}) collective-permute-start(f32[2,64,128]{2,1,0:T(8,128)S(1)} %get-tuple-element.52.s0), channel_id=1, source_target_pairs={{0,8},{2,10},{4,12},{6,14},{8,0},{10,2},{12,4},{14,6},{1,9},{3,11}... | collective-permute-start | bytes 196616 | tf_op jit(solution)/shard_map/ppermute | solution.py:362
  78.2 1.7 %collective-permute-start.15 = (f32[2,64,128]{2,1,0:T(8,128)S(1)}, f32[2,64,128]{2,1,0:T(8,128)S(1)}, u32[]{:S(2)}, u32[]{:S(2)}) collective-permute-start(f32[2,64,128]{2,1,0:T(8,128)S(1)} %get-tuple-element.52.s0), channel_id=1, source_target_pairs={{0,12},{2,14},{4,8},{6,10},{8,4},{10,6},{12,0},{14,2},{1,13},{3,15... | collective-permute-start | bytes 196616 | tf_op jit(solution)/shard_map/ppermute | solution.py:362
  79.8 3.9 %collective-permute-done.14.s2 = f32[2,64,128]{2,1,0:T(8,128)S(1)} collective-permute-done((f32[2,64,128]{2,1,0:T(8,128)S(1)}, f32[2,64,128]{2,1,0:T(8,128)S(1)}, u32[]{:S(2)}, u32[]{:S(2)}) %collective-permute-start.14) | collective-permute-done | bytes 65568 | tf_op jit(solution)/shard_map/ppermute | solution.py:362
  83.8 1.4 collective-permute-done.15.s3
  85.2 3.3 %collective-permute-start.16 = (f32[8,64,128]{2,1,0:T(8,128)S(1)}, f32[8,64,128]{2,1,0:T(8,128)S(1)}, u32[]{:S(2)}, u32[]{:S(2)}) collective-permute-start(f32[8,64,128]{2,1,0:T(8,128)S(1)} %shard_map.100.az), channel_id=1, source_target_pairs={{0,1},{1,0},{2,3},{3,2},{4,5},{5,4},{6,7},{7,6},{8,9},{9,8},{10,11... | collective-permute-start | bytes 786440 | tf_op jit(solution)/shard_map/ppermute | solution.py:350
  88.5 1.2 collective-permute-done.16.ao
  89.6 2.9 %shard_map.101 = (f32[8,64,128]{2,1,0:T(8,128)S(1)}, f32[9,64,128]{2,1,0:T(8,128)S(1)}, f32[16,64,128]{2,1,0:T(8,128)}, f32[4,128,128]{2,1,0:T(8,128)S(1)}, f32[...) custom-call(s32[3,4]{1,0:T(4,128)S(1)} %copy-done.2, s32[1]{0:T(128)S(6)} %copy.10.counts, s32[1]{0:T(128)} %bitcast.1.code_ref, ...), custom_call_target="tpu_custom_call" | custom-call | tf_op jit(solution)/shard_map/pallas_call | solution.py:47
  92.9 6.6 %all-to-all-start.4 = ((f32[16,64,128]{2,1,0:T(8,128)}), f32[16,64,128]{2,1,0:T(8,128)S(1)}, u32[]{:S(2)}, u32[]{:S(2)}) async-start(f32[16,64,128]{2,1,0:T(8,128)} %get-tuple-element.61), calls=%async_computation.4 | async-start | bytes 1048576 | tf_op jit(solution)/shard_map/all_to_all | solution.py:346
  99.6 1.4 collective-permute-start.18
  100.9 3.9 %collective-permute-start.19 = (f32[136,128]{1,0:T(8,128)S(1)}, f32[136,128]{1,0:T(8,128)S(1)}, u32[]{:S(2)}, u32[]{:S(2)}) collective-permute-start(f32[136,128]{1,0:T(8,128)S(1)} %get-tuple-element.78), channel_id=1, source_target_pairs={{0,8},{2,10},{4,12},{6,14},{8,0},{10,2},{12,4},{14,6},{1,9},{3,11}... | collective-permute-start | bytes 208904 | tf_op jit(solution)/shard_map/ppermute | solution.py:362
  105.3 3.0 %collective-permute-done.19.s2 = f32[136,128]{1,0:T(8,128)S(1)} collective-permute-done((f32[136,128]{1,0:T(8,128)S(1)}, f32[136,128]{1,0:T(8,128)S(1)}, u32[]{:S(2)}, u32[]{:S(2)}) %collective-permute-start.19) | collective-permute-done | bytes 69664 | tf_op jit(solution)/shard_map/ppermute | solution.py:362
  108.3 2.4 %collective-permute-done.20.s3 = f32[136,128]{1,0:T(8,128)S(1)} collective-permute-done((f32[136,128]{1,0:T(8,128)S(1)}, f32[136,128]{1,0:T(8,128)S(1)}, u32[]{:S(2)}, u32[]{:S(2)}) %collective-permute-start.20) | collective-permute-done | bytes 69664 | tf_op jit(solution)/shard_map/ppermute | solution.py:362
  110.8 3.3 %collective-permute-start.21 = (f32[160,128]{1,0:T(8,128)S(1)}, f32[160,128]{1,0:T(8,128)S(1)}, u32[]{:S(2)}, u32[]{:S(2)}) collective-permute-start(f32[160,128]{1,0:T(8,128)S(1)} %shard_map.103.mine), channel_id=1, source_target_pairs={{0,2},{2,0},{4,6},{6,4},{8,10},{10,8},{12,14},{14,12},{1,3},{3,1},... | collective-permute-start | bytes 245768 | tf_op jit(solution)/shard_map/ppermute | solution.py:366
  114.1 2.3 %collective-permute-done.21.received = f32[160,128]{1,0:T(8,128)S(1)} collective-permute-done((f32[160,128]{1,0:T(8,128)S(1)}, f32[160,128]{1,0:T(8,128)S(1)}, u32[]{:S(2)}, u32[]{:S(2)}) %collective-permute-start.21) | collective-permute-done | bytes 81952 | tf_op jit(solution)/shard_map/ppermute | solution.py:366
  117.4 6.8 %all-to-all-start.5 = ((f32[16,104,128]{2,1,0:T(8,128)}), f32[16,104,128]{2,1,0:T(8,128)S(1)}, u32[]{:S(2)}, u32[]{:S(2)}) async-start(f32[16,104,128]{2,1,0:T(8,128)} %get-tuple-element.63), calls=%async_computation.5 | async-start | bytes 1703936 | tf_op jit(solution)/shard_map/all_to_all | solution.py:346
  124.2 1.6 collective-permute-start.22
  125.8 2.3 %collective-permute-start.23 = (f32[2,64,128]{2,1,0:T(8,128)S(1)}, f32[2,64,128]{2,1,0:T(8,128)S(1)}, u32[]{:S(2)}, u32[]{:S(2)}) collective-permute-start(f32[2,64,128]{2,1,0:T(8,128)S(1)} %get-tuple-element.62.s0), channel_id=1, source_target_pairs={{0,8},{2,10},{4,12},{6,14},{8,0},{10,2},{12,4},{14,6},{1,9},{3,11}... | collective-permute-start | bytes 196616 | tf_op jit(solution)/shard_map/ppermute | solution.py:362
  128.1 1.8 %collective-permute-start.24 = (f32[2,64,128]{2,1,0:T(8,128)S(1)}, f32[2,64,128]{2,1,0:T(8,128)S(1)}, u32[]{:S(2)}, u32[]{:S(2)}) collective-permute-start(f32[2,64,128]{2,1,0:T(8,128)S(1)} %get-tuple-element.62.s0), channel_id=1, source_target_pairs={{0,12},{2,14},{4,8},{6,10},{8,4},{10,6},{12,0},{14,2},{1,13},{3,15... | collective-permute-start | bytes 196616 | tf_op jit(solution)/shard_map/ppermute | solution.py:362
  129.9 3.6 %collective-permute-done.23.s2 = f32[2,64,128]{2,1,0:T(8,128)S(1)} collective-permute-done((f32[2,64,128]{2,1,0:T(8,128)S(1)}, f32[2,64,128]{2,1,0:T(8,128)S(1)}, u32[]{:S(2)}, u32[]{:S(2)}) %collective-permute-start.23) | collective-permute-done | bytes 65568 | tf_op jit(solution)/shard_map/ppermute | solution.py:362
  134.7 3.0 %collective-permute-start.25 = (f32[8,64,128]{2,1,0:T(8,128)S(1)}, f32[8,64,128]{2,1,0:T(8,128)S(1)}, u32[]{:S(2)}, u32[]{:S(2)}) collective-permute-start(f32[8,64,128]{2,1,0:T(8,128)S(1)} %shard_map.105.az), channel_id=1, source_target_pairs={{0,1},{1,0},{2,3},{3,2},{4,5},{5,4},{6,7},{7,6},{8,9},{9,8},{10,11... | collective-permute-start | bytes 786440 | tf_op jit(solution)/shard_map/ppermute | solution.py:350
  137.7 1.2 collective-permute-done.25.ao
  138.8 2.4 %shard_map.106 = (f32[64,128]{1,0:T(8,128)S(1)}, f32[64,128]{1,0:T(8,128)S(1)}, f32[64,128]{1,0:T(8,128)S(1)}, f32[8,128]{1,0:T(8,128)S(1)}, f32[256,1,128]{2,1,0:T(1,128)}) custom-call(s32[3,4]{1,0:T(4,128)S(1)} %copy-done.2, s32[1]{0:T(128)S(6)} %copy.10.counts, s32[1]{0:T(128)} %bitcast.1.code_ref, f32[8,64,128]{2,1,0:T(8,128)S(1)} %shard_map.105.az, ...), custom_call_target="tpu_custom_call" | custom-call | tf_op jit(solution)/shard_map/pallas_call | solution.py:47
  141.2 10.6 %all-to-all-start.6 = ((f32[256,1,128]{2,1,0:T(1,128)}), f32[256,1,128]{2,1,0:T(1,128)S(1)}, u32[]{:S(2)}, u32[]{:S(2)}) async-start(f32[256,1,128]{2,1,0:T(1,128)} %get-tuple-element.69), calls=%async_computation.6 | async-start | bytes 262144 | tf_op jit(solution)/shard_map/all_to_all | solution.py:424
  152.4 12.2 %all-to-all-done.6 = f32[256,1,128]{2,1,0:T(1,128)S(1)} async-done(((f32[256,1,128]{2,1,0:T(1,128)}), f32[256,1,128]{2,1,0:T(1,128)S(1)}, u32[]{:S(2)}, u32[]{:S(2)}) %all-to-all-start.6) | async-done | bytes 131104 | tf_op jit(solution)/shard_map/all_to_all | solution.py:424
  (41 shorter events, 7.9 us)
Async XLA Ops:
  2.2 9.1 %copy-start.1 = (f32[64,128]{1,0:T(8,128)S(1)}, f32[64,128]{1,0:T(8,128)}, u32[]{:S(2)}) copy-start(f32[64,128]{1,0:T(8,128)} %get-tuple-element.41.b0) | copy-start | bytes 98308
  2.2 20.4 %all-to-all-start = ((f32[8,72,128]{2,1,0:T(8,128)}), f32[8,72,128]{2,1,0:T(8,128)S(1)}, u32[]{:S(2)}, u32[]{:S(2)}) async-start(f32[8,72,128]{2,1,0:T(8,128)} %get-tuple-element.40), calls=%async_computation | async-start | bytes 589824 | tf_op jit(solution)/shard_map/all_to_all | solution.py:342
  11.3 3.9 %collective-permute-start.1 = (f32[64,128]{1,0:T(8,128)S(1)}, f32[64,128]{1,0:T(8,128)S(1)}, u32[]{:S(2)}, u32[]{:S(2)}) collective-permute-start(f32[64,128]{1,0:T(8,128)S(1)} %copy-done.1), channel_id=1, source_target_pairs={{0,16},{16,0},{32,48},{48,32},{1,17},{17,1},{33,49},{49,33},{2,18}... | collective-permute-start | bytes 98312 | tf_op jit(solution)/shard_map/ppermute | solution.py:354
  12.6 4.3 %collective-permute-start.2 = (f32[64,128]{1,0:T(8,128)S(1)}, f32[64,128]{1,0:T(8,128)S(1)}, u32[]{:S(2)}, u32[]{:S(2)}) collective-permute-start(f32[64,128]{1,0:T(8,128)S(1)} %copy-done.1), channel_id=1, source_target_pairs={{0,32},{16,48},{32,0},{48,16},{1,33},{17,49},{33,1},{49,17},{2,34}... | collective-permute-start | bytes 98312 | tf_op jit(solution)/shard_map/ppermute | solution.py:354
  15.0 4.3 %collective-permute-start.3 = (f32[64,128]{1,0:T(8,128)S(1)}, f32[64,128]{1,0:T(8,128)S(1)}, u32[]{:S(2)}, u32[]{:S(2)}) collective-permute-start(f32[64,128]{1,0:T(8,128)S(1)} %copy-done.1), channel_id=1, source_target_pairs={{0,48},{16,32},{32,16},{48,0},{1,49},{17,33},{33,17},{49,1},{2,50}... | collective-permute-start | bytes 98312 | tf_op jit(solution)/shard_map/ppermute | solution.py:354
  23.3 22.9 %copy-start = (bf16[4,128,128]{2,1,0:T(8,128)(2,1)S(1)}, bf16[4,128,128]{2,1,0:T(8,128)(2,1)}, u32[]{:S(2)}) copy-start(bf16[4,128,128]{2,1,0:T(8,128)(2,1)} %data.1) | copy-start | bytes 393220
  23.4 20.1 %all-to-all-start.1 = ((f32[16,32,128]{2,1,0:T(8,128)}), f32[16,32,128]{2,1,0:T(8,128)S(1)}, u32[]{:S(2)}, u32[]{:S(2)}) async-start(f32[16,32,128]{2,1,0:T(8,128)} %get-tuple-element.42), calls=%async_computation.1 | async-start | bytes 524288 | tf_op jit(solution)/shard_map/all_to_all | solution.py:346
  30.2 7.3 %collective-permute-start.4 = (f32[4,64,128]{2,1,0:T(8,128)S(1)}, f32[4,64,128]{2,1,0:T(8,128)S(1)}, u32[]{:S(2)}, u32[]{:S(2)}) collective-permute-start(f32[4,64,128]{2,1,0:T(8,128)S(1)} %get-tuple-element.44.b0), channel_id=1, source_target_pairs={{0,64},{64,0},{128,192},{192,128},{1,65},{65,1},{129,193},{193,129... | collective-permute-start | bytes 393224 | tf_op jit(solution)/shard_map/ppermute | solution.py:354
  31.6 9.5 %collective-permute-start.5 = (f32[4,64,128]{2,1,0:T(8,128)S(1)}, f32[4,64,128]{2,1,0:T(8,128)S(1)}, u32[]{:S(2)}, u32[]{:S(2)}) collective-permute-start(f32[4,64,128]{2,1,0:T(8,128)S(1)} %get-tuple-element.44.b0), channel_id=1, source_target_pairs={{0,128},{64,192},{128,0},{192,64},{1,129},{65,193},{129,1},{193,65... | collective-permute-start | bytes 393224 | tf_op jit(solution)/shard_map/ppermute | solution.py:354
  34.0 9.4 %collective-permute-start.6 = (f32[4,64,128]{2,1,0:T(8,128)S(1)}, f32[4,64,128]{2,1,0:T(8,128)S(1)}, u32[]{:S(2)}, u32[]{:S(2)}) collective-permute-start(f32[4,64,128]{2,1,0:T(8,128)S(1)} %get-tuple-element.44.b0), channel_id=1, source_target_pairs={{0,192},{64,128},{128,64},{192,0},{1,193},{65,129},{129,65},{193,1... | collective-permute-start | bytes 393224 | tf_op jit(solution)/shard_map/ppermute | solution.py:354
  34.2 11.6 %collective-permute-start = (f32[8,72,128]{2,1,0:T(8,128)S(1)}, f32[8,72,128]{2,1,0:T(8,128)S(1)}, u32[]{:S(2)}, u32[]{:S(2)}) collective-permute-start(f32[8,72,128]{2,1,0:T(8,128)S(1)} %all-to-all-done.gz), channel_id=1, source_target_pairs={{0,1},{1,0},{2,3},{3,2},{4,5},{5,4},{6,7},{7,6},{8,9},{9,8},{10,11... | collective-permute-start | bytes 884744 | tf_op jit(solution)/shard_map/ppermute | solution.py:350
  43.4 2.8 %collective-permute-start.7 = (f32[16,32,128]{2,1,0:T(8,128)S(1)}, f32[16,32,128]{2,1,0:T(8,128)S(1)}, u32[]{:S(2)}, u32[]{:S(2)}) collective-permute-start(f32[16,32,128]{2,1,0:T(8,128)S(1)} %all-to-all-done.1.gr), channel_id=1, source_target_pairs={{0,1},{1,0},{2,3},{3,2},{4,5},{5,4},{6,7},{7,6},{8,9},{9,8},{10,11... | collective-permute-start | bytes 786440 | tf_op jit(solution)/shard_map/ppermute | solution.py:350
  45.8 0.7 copy-start.2
  48.8 4.2 %collective-permute-start.8 = (f32[9,64,128]{2,1,0:T(8,128)S(1)}, f32[9,64,128]{2,1,0:T(8,128)S(1)}, u32[]{:S(2)}, u32[]{:S(2)}) collective-permute-start(f32[9,64,128]{2,1,0:T(8,128)S(1)} %get-tuple-element.50.send), channel_id=1, source_target_pairs={{0,1},{1,0},{2,3},{3,2},{4,5},{5,4},{6,7},{7,6},{8,9},{9,8},{10,11... | collective-permute-start | bytes 884744 | tf_op jit(solution)/shard_map/ppermute | solution.py:350
  49.0 16.9 %all-to-all-start.2 = ((f32[16,64,128]{2,1,0:T(8,128)}), f32[16,64,128]{2,1,0:T(8,128)S(1)}, u32[]{:S(2)}, u32[]{:S(2)}) async-start(f32[16,64,128]{2,1,0:T(8,128)} %get-tuple-element.51), calls=%async_computation.2 | async-start | bytes 1048576 | tf_op jit(solution)/shard_map/all_to_all | solution.py:346
  53.1 7.3 %collective-permute-start.10 = (f32[136,128]{1,0:T(8,128)S(1)}, f32[136,128]{1,0:T(8,128)S(1)}, u32[]{:S(2)}, u32[]{:S(2)}) collective-permute-start(f32[136,128]{1,0:T(8,128)S(1)} %get-tuple-element.81), channel_id=1, source_target_pairs={{0,8},{2,10},{4,12},{6,14},{8,0},{10,2},{12,4},{14,6},{1,9},{3,11}... | collective-permute-start | bytes 208904 | tf_op jit(solution)/shard_map/ppermute | solution.py:362
  54.3 6.4 %collective-permute-start.11 = (f32[136,128]{1,0:T(8,128)S(1)}, f32[136,128]{1,0:T(8,128)S(1)}, u32[]{:S(2)}, u32[]{:S(2)}) collective-permute-start(f32[136,128]{1,0:T(8,128)S(1)} %get-tuple-element.80), channel_id=1, source_target_pairs={{0,12},{2,14},{4,8},{6,10},{8,4},{10,6},{12,0},{14,2},{1,13},{3,15... | collective-permute-start | bytes 208904 | tf_op jit(solution)/shard_map/ppermute | solution.py:362
  56.0 4.9 %collective-permute-start.9 = (f32[136,128]{1,0:T(8,128)S(1)}, f32[136,128]{1,0:T(8,128)S(1)}, u32[]{:S(2)}, u32[]{:S(2)}) collective-permute-start(f32[136,128]{1,0:T(8,128)S(1)} %get-tuple-element.82), channel_id=1, source_target_pairs={{0,4},{2,6},{4,0},{6,2},{8,12},{10,14},{12,8},{14,10},{1,5},{3,7},... | collective-permute-start | bytes 208904 | tf_op jit(solution)/shard_map/ppermute | solution.py:362
  60.9 5.0 %collective-permute-start.12 = (f32[160,128]{1,0:T(8,128)S(1)}, f32[160,128]{1,0:T(8,128)S(1)}, u32[]{:S(2)}, u32[]{:S(2)}) collective-permute-start(f32[160,128]{1,0:T(8,128)S(1)} %shard_map.98.mine), channel_id=1, source_target_pairs={{0,2},{2,0},{4,6},{6,4},{8,10},{10,8},{12,14},{14,12},{1,3},{3,1},... | collective-permute-start | bytes 245768 | tf_op jit(solution)/shard_map/ppermute | solution.py:366
  66.9 22.7 %all-to-all-start.3 = ((f32[16,104,128]{2,1,0:T(8,128)}), f32[16,104,128]{2,1,0:T(8,128)S(1)}, u32[]{:S(2)}, u32[]{:S(2)}) async-start(f32[16,104,128]{2,1,0:T(8,128)} %get-tuple-element.53), calls=%async_computation.3 | async-start | bytes 1703936 | tf_op jit(solution)/shard_map/all_to_all | solution.py:346
  72.8 7.1 %collective-permute-start.13 = (f32[2,64,128]{2,1,0:T(8,128)S(1)}, f32[2,64,128]{2,1,0:T(8,128)S(1)}, u32[]{:S(2)}, u32[]{:S(2)}) collective-permute-start(f32[2,64,128]{2,1,0:T(8,128)S(1)} %get-tuple-element.52.s0), channel_id=1, source_target_pairs={{0,4},{2,6},{4,0},{6,2},{8,12},{10,14},{12,8},{14,10},{1,5},{3,7},... | collective-permute-start | bytes 196616 | tf_op jit(solution)/shard_map/ppermute | solution.py:362
  76.5 7.3 %collective-permute-start.14 = (f32[2,64,128]{2,1,0:T(8,128)S(1)}, f32[2,64,128]{2,1,0:T(8,128)S(1)}, u32[]{:S(2)}, u32[]{:S(2)}) collective-permute-start(f32[2,64,128]{2,1,0:T(8,128)S(1)} %get-tuple-element.52.s0), channel_id=1, source_target_pairs={{0,8},{2,10},{4,12},{6,14},{8,0},{10,2},{12,4},{14,6},{1,9},{3,11}... | collective-permute-start | bytes 196616 | tf_op jit(solution)/shard_map/ppermute | solution.py:362
  78.2 7.0 %collective-permute-start.15 = (f32[2,64,128]{2,1,0:T(8,128)S(1)}, f32[2,64,128]{2,1,0:T(8,128)S(1)}, u32[]{:S(2)}, u32[]{:S(2)}) collective-permute-start(f32[2,64,128]{2,1,0:T(8,128)S(1)} %get-tuple-element.52.s0), channel_id=1, source_target_pairs={{0,12},{2,14},{4,8},{6,10},{8,4},{10,6},{12,0},{14,2},{1,13},{3,15... | collective-permute-start | bytes 196616 | tf_op jit(solution)/shard_map/ppermute | solution.py:362
  85.2 4.4 %collective-permute-start.16 = (f32[8,64,128]{2,1,0:T(8,128)S(1)}, f32[8,64,128]{2,1,0:T(8,128)S(1)}, u32[]{:S(2)}, u32[]{:S(2)}) collective-permute-start(f32[8,64,128]{2,1,0:T(8,128)S(1)} %shard_map.100.az), channel_id=1, source_target_pairs={{0,1},{1,0},{2,3},{3,2},{4,5},{5,4},{6,7},{7,6},{8,9},{9,8},{10,11... | collective-permute-start | bytes 786440 | tf_op jit(solution)/shard_map/ppermute | solution.py:350
  92.5 7.0 %collective-permute-start.17 = (f32[9,64,128]{2,1,0:T(8,128)S(1)}, f32[9,64,128]{2,1,0:T(8,128)S(1)}, u32[]{:S(2)}, u32[]{:S(2)}) collective-permute-start(f32[9,64,128]{2,1,0:T(8,128)S(1)} %get-tuple-element.60.send), channel_id=1, source_target_pairs={{0,1},{1,0},{2,3},{3,2},{4,5},{5,4},{6,7},{7,6},{8,9},{9,8},{10,11... | collective-permute-start | bytes 884744 | tf_op jit(solution)/shard_map/ppermute | solution.py:350
  92.9 23.5 %all-to-all-start.4 = ((f32[16,64,128]{2,1,0:T(8,128)}), f32[16,64,128]{2,1,0:T(8,128)S(1)}, u32[]{:S(2)}, u32[]{:S(2)}) async-start(f32[16,64,128]{2,1,0:T(8,128)} %get-tuple-element.61), calls=%async_computation.4 | async-start | bytes 1048576 | tf_op jit(solution)/shard_map/all_to_all | solution.py:346
  99.6 5.7 %collective-permute-start.18 = (f32[136,128]{1,0:T(8,128)S(1)}, f32[136,128]{1,0:T(8,128)S(1)}, u32[]{:S(2)}, u32[]{:S(2)}) collective-permute-start(f32[136,128]{1,0:T(8,128)S(1)} %get-tuple-element.79), channel_id=1, source_target_pairs={{0,4},{2,6},{4,0},{6,2},{8,12},{10,14},{12,8},{14,10},{1,5},{3,7},... | collective-permute-start | bytes 208904 | tf_op jit(solution)/shard_map/ppermute | solution.py:362
  100.9 7.4 %collective-permute-start.19 = (f32[136,128]{1,0:T(8,128)S(1)}, f32[136,128]{1,0:T(8,128)S(1)}, u32[]{:S(2)}, u32[]{:S(2)}) collective-permute-start(f32[136,128]{1,0:T(8,128)S(1)} %get-tuple-element.78), channel_id=1, source_target_pairs={{0,8},{2,10},{4,12},{6,14},{8,0},{10,2},{12,4},{14,6},{1,9},{3,11}... | collective-permute-start | bytes 208904 | tf_op jit(solution)/shard_map/ppermute | solution.py:362
  104.8 5.9 %collective-permute-start.20 = (f32[136,128]{1,0:T(8,128)S(1)}, f32[136,128]{1,0:T(8,128)S(1)}, u32[]{:S(2)}, u32[]{:S(2)}) collective-permute-start(f32[136,128]{1,0:T(8,128)S(1)} %get-tuple-element.77), channel_id=1, source_target_pairs={{0,12},{2,14},{4,8},{6,10},{8,4},{10,6},{12,0},{14,2},{1,13},{3,15... | collective-permute-start | bytes 208904 | tf_op jit(solution)/shard_map/ppermute | solution.py:362
  110.8 5.6 %collective-permute-start.21 = (f32[160,128]{1,0:T(8,128)S(1)}, f32[160,128]{1,0:T(8,128)S(1)}, u32[]{:S(2)}, u32[]{:S(2)}) collective-permute-start(f32[160,128]{1,0:T(8,128)S(1)} %shard_map.103.mine), channel_id=1, source_target_pairs={{0,2},{2,0},{4,6},{6,4},{8,10},{10,8},{12,14},{14,12},{1,3},{3,1},... | collective-permute-start | bytes 245768 | tf_op jit(solution)/shard_map/ppermute | solution.py:366
  117.4 21.5 %all-to-all-start.5 = ((f32[16,104,128]{2,1,0:T(8,128)}), f32[16,104,128]{2,1,0:T(8,128)S(1)}, u32[]{:S(2)}, u32[]{:S(2)}) async-start(f32[16,104,128]{2,1,0:T(8,128)} %get-tuple-element.63), calls=%async_computation.5 | async-start | bytes 1703936 | tf_op jit(solution)/shard_map/all_to_all | solution.py:346
  124.2 5.7 %collective-permute-start.22 = (f32[2,64,128]{2,1,0:T(8,128)S(1)}, f32[2,64,128]{2,1,0:T(8,128)S(1)}, u32[]{:S(2)}, u32[]{:S(2)}) collective-permute-start(f32[2,64,128]{2,1,0:T(8,128)S(1)} %get-tuple-element.62.s0), channel_id=1, source_target_pairs={{0,4},{2,6},{4,0},{6,2},{8,12},{10,14},{12,8},{14,10},{1,5},{3,7},... | collective-permute-start | bytes 196616 | tf_op jit(solution)/shard_map/ppermute | solution.py:362
  125.8 7.7 %collective-permute-start.23 = (f32[2,64,128]{2,1,0:T(8,128)S(1)}, f32[2,64,128]{2,1,0:T(8,128)S(1)}, u32[]{:S(2)}, u32[]{:S(2)}) collective-permute-start(f32[2,64,128]{2,1,0:T(8,128)S(1)} %get-tuple-element.62.s0), channel_id=1, source_target_pairs={{0,8},{2,10},{4,12},{6,14},{8,0},{10,2},{12,4},{14,6},{1,9},{3,11}... | collective-permute-start | bytes 196616 | tf_op jit(solution)/shard_map/ppermute | solution.py:362
  128.1 6.5 %collective-permute-start.24 = (f32[2,64,128]{2,1,0:T(8,128)S(1)}, f32[2,64,128]{2,1,0:T(8,128)S(1)}, u32[]{:S(2)}, u32[]{:S(2)}) collective-permute-start(f32[2,64,128]{2,1,0:T(8,128)S(1)} %get-tuple-element.62.s0), channel_id=1, source_target_pairs={{0,12},{2,14},{4,8},{6,10},{8,4},{10,6},{12,0},{14,2},{1,13},{3,15... | collective-permute-start | bytes 196616 | tf_op jit(solution)/shard_map/ppermute | solution.py:362
  134.7 4.1 %collective-permute-start.25 = (f32[8,64,128]{2,1,0:T(8,128)S(1)}, f32[8,64,128]{2,1,0:T(8,128)S(1)}, u32[]{:S(2)}, u32[]{:S(2)}) collective-permute-start(f32[8,64,128]{2,1,0:T(8,128)S(1)} %shard_map.105.az), channel_id=1, source_target_pairs={{0,1},{1,0},{2,3},{3,2},{4,5},{5,4},{6,7},{7,6},{8,9},{9,8},{10,11... | collective-permute-start | bytes 786440 | tf_op jit(solution)/shard_map/ppermute | solution.py:350
  141.2 23.4 %all-to-all-start.6 = ((f32[256,1,128]{2,1,0:T(1,128)}), f32[256,1,128]{2,1,0:T(1,128)S(1)}, u32[]{:S(2)}, u32[]{:S(2)}) async-start(f32[256,1,128]{2,1,0:T(1,128)} %get-tuple-element.69), calls=%async_computation.6 | async-start | bytes 262144 | tf_op jit(solution)/shard_map/all_to_all | solution.py:424
where the time goes:
time: 167 us; the launch traced here: 166 us
  starting transfers between devices  100 us (60%)
  waiting for transfers between devices  49.9 us (30%)
  Pallas kernels  12.9 us (8%)
  between operations  2.07 us (1%)
    all_to_all x5, starting transfers between devices, along_row(): return lax.all_to_all(x, ROW, 0, 0, tiled=True)  30 us
    ppermute x12, starting transfers between devices, pair_shift(): return lax.ppermute(x, 'z', [(i, i ^ 2 * k) for i in range(8)])  24.3 us
    ppermute x12, waiting for transfers between devices, pair_shift(): return lax.ppermute(x, 'z', [(i, i ^ 2 * k) for i in range(8)])  17.5 us
    pallas_call x14, Pallas kernels, call(): pl.pallas_call(body, out_shape=outs, in_specs=[SMEM] * scalars + [VMEM] *...  12.9 us
    all_to_all x1, waiting for transfers between devices, step_of(): sums = jnp.sum(lax.all_to_all(spread, ALL, 0, 0, tiled=True), axis=0)  12.2 us
    ppermute x6, starting transfers between devices, swap(): return lax.ppermute(x, 'c', [(0, 1), (1, 0)])  11.9 us
    all_to_all x1, starting transfers between devices, step_of(): sums = jnp.sum(lax.all_to_all(spread, ALL, 0, 0, tiled=True), axis=0)  10.6 us
    ppermute x6, waiting for transfers between devices, shift(): return lax.ppermute(x, axis, [(i, i ^ k) for i in range(4)])  9.93 us
  transfers between devices with their start and end apart: 33, of which 20 were waited for; matrix products, arithmetic and copies ran while one was open for 0% of the time, Pallas kernels for 0%

commit v1 on v0

--- a/solution.py
+++ b/solution.py
@@ -369,7 +369,9 @@
 def shares(keep, send, fb, scalars):
     joined = call(join_body, shaped(4, 2 * R + 8, T), (keep, send, swap(send)))
     gr = along_row(fb)
-    strides = tuple(pair_shift(joined[k], k) for k in range(1, 4))
+    strides = []
+    for k in range(1, 4):
+        strides.append(pair_shift(joined[k], k))
     mine = call(
         pair_body,
         shaped(2 * R + 32, T),
@@ -398,7 +400,10 @@
         turn_body, (shaped(NP, 32, T), shaped(4, R, T)), (gz, fc, *from_near(fc, "x"))
     )
     gr = along_row(payload)
-    gr, *stacks = lax.optimization_barrier((gr, stack, *from_near(stack, "y")))
+    below = []
+    for k in range(1, 4):
+        below.append(shift(stack, "y", k))
+    gr, *stacks = lax.optimization_barrier((gr, stack, *below))
     folded = (shaped(NZ, R, T), shaped(NZ + 1, R, T), shaped(NP, R, T))
     saved = (shaped(TILES, R, T), shaped(TILES, R, T), shaped(R, T))
     keep, send, fb, ta, tb, tc = call(

time: 167 us -> 167 us (level)
  no operation moved by 1% of the time
where the time goes in v1:
time: 167 us; the launch traced here: 166 us
  starting transfers between devices  100 us (60%)
  waiting for transfers between devices  49.9 us (30%)
  Pallas kernels  12.9 us (8%)
  between operations  2.07 us (1%)
    all_to_all x5, starting transfers between devices, along_row(): return lax.all_to_all(x, ROW, 0, 0, tiled=True)  30 us
    ppermute x12, starting transfers between devices, pair_shift(): return lax.ppermute(x, 'z', [(i, i ^ 2 * k) for i in range(8)])  24.3 us
    ppermute x12, waiting for transfers between devices, pair_shift(): return lax.ppermute(x, 'z', [(i, i ^ 2 * k) for i in range(8)])  17.5 us
    pallas_call x14, Pallas kernels, call(): pl.pallas_call(body, out_shape=outs, in_specs=[SMEM] * scalars + [VMEM] *...  12.9 us
    all_to_all x1, waiting for transfers between devices, step_of(): sums = jnp.sum(lax.all_to_all(spread, ALL, 0, 0, tiled=True), axis=0)  12.2 us
    ppermute x6, starting transfers between devices, swap(): return lax.ppermute(x, 'c', [(0, 1), (1, 0)])  11.9 us
    all_to_all x1, starting transfers between devices, step_of(): sums = jnp.sum(lax.all_to_all(spread, ALL, 0, 0, tiled=True), axis=0)  10.6 us
    ppermute x6, waiting for transfers between devices, shift(): return lax.ppermute(x, axis, [(i, i ^ k) for i in range(4)])  9.93 us
  transfers between devices with their start and end apart: 33, of which 20 were waited for; matrix products, arithmetic and copies ran while one was open for 0% of the time, Pallas kernels for 0%

profile of v1, /device:TPU:1, one launch (start us, length us, event | category | flops | bytes accessed | tf_op | source)
XLA Modules:
  0.0 165.7 jit_solution(2238928730570318652)
XLA Ops:
  0.6 1.5 shard_map.94
  2.2 9.1 %all-to-all-start = ((f32[8,72,128]{2,1,0:T(8,128)}), f32[8,72,128]{2,1,0:T(8,128)S(1)}, u32[]{:S(2)}, u32[]{:S(2)}) async-start(f32[8,72,128]{2,1,0:T(8,128)} %get-tuple-element.40), calls=%async_computation | async-start | bytes 589824 | tf_op jit(solution)/shard_map/all_to_all | solution.py:342
  11.3 1.3 collective-permute-start.1
  12.6 2.5 %collective-permute-start.2 = (f32[64,128]{1,0:T(8,128)S(1)}, f32[64,128]{1,0:T(8,128)S(1)}, u32[]{:S(2)}, u32[]{:S(2)}) collective-permute-start(f32[64,128]{1,0:T(8,128)S(1)} %copy-done.1), channel_id=1, source_target_pairs={{0,32},{16,48},{32,0},{48,16},{1,33},{17,49},{33,1},{49,17},{2,34}... | collective-permute-start | bytes 98312 | tf_op jit(solution)/shard_map/ppermute | solution.py:354
  15.2 1.6 collective-permute-done.2.b2
  16.9 2.5 %collective-permute-done.3.b3 = f32[64,128]{1,0:T(8,128)S(1)} collective-permute-done((f32[64,128]{1,0:T(8,128)S(1)}, f32[64,128]{1,0:T(8,128)S(1)}, u32[]{:S(2)}, u32[]{:S(2)}) %collective-permute-start.3) | collective-permute-done | bytes 32800 | tf_op jit(solution)/shard_map/ppermute | solution.py:354
  19.3 3.2 %all-to-all-done.gz = f32[8,72,128]{2,1,0:T(8,128)S(1)} async-done(((f32[8,72,128]{2,1,0:T(8,128)}), f32[8,72,128]{2,1,0:T(8,128)S(1)}, u32[]{:S(2)}, u32[]{:S(2)}) %all-to-all-start) | async-done | bytes 294944 | tf_op jit(solution)/shard_map/all_to_all | solution.py:342
  23.4 6.9 %all-to-all-start.1 = ((f32[16,32,128]{2,1,0:T(8,128)}), f32[16,32,128]{2,1,0:T(8,128)S(1)}, u32[]{:S(2)}, u32[]{:S(2)}) async-start(f32[16,32,128]{2,1,0:T(8,128)} %get-tuple-element.42), calls=%async_computation.1 | async-start | bytes 524288 | tf_op jit(solution)/shard_map/all_to_all | solution.py:346
  30.2 1.4 collective-permute-start.4
  31.6 2.4 %collective-permute-start.5 = (f32[4,64,128]{2,1,0:T(8,128)S(1)}, f32[4,64,128]{2,1,0:T(8,128)S(1)}, u32[]{:S(2)}, u32[]{:S(2)}) collective-permute-start(f32[4,64,128]{2,1,0:T(8,128)S(1)} %get-tuple-element.44.b0), channel_id=1, source_target_pairs={{0,128},{64,192},{128,0},{192,64},{1,129},{65,193},{129,1},{193,65... | collective-permute-start | bytes 393224 | tf_op jit(solution)/shard_map/ppermute | solution.py:354
  34.2 3.4 %collective-permute-start = (f32[8,72,128]{2,1,0:T(8,128)S(1)}, f32[8,72,128]{2,1,0:T(8,128)S(1)}, u32[]{:S(2)}, u32[]{:S(2)}) collective-permute-start(f32[8,72,128]{2,1,0:T(8,128)S(1)} %all-to-all-done.gz), channel_id=1, source_target_pairs={{0,1},{1,0},{2,3},{3,2},{4,5},{5,4},{6,7},{7,6},{8,9},{9,8},{10,11... | collective-permute-start | bytes 884744 | tf_op jit(solution)/shard_map/ppermute | solution.py:350
  37.6 3.5 %collective-permute-done.5.b2 = f32[4,64,128]{2,1,0:T(8,128)S(1)} collective-permute-done((f32[4,64,128]{2,1,0:T(8,128)S(1)}, f32[4,64,128]{2,1,0:T(8,128)S(1)}, u32[]{:S(2)}, u32[]{:S(2)}) %collective-permute-start.5) | collective-permute-done | bytes 131104 | tf_op jit(solution)/shard_map/ppermute | solution.py:354
  41.1 2.3 %collective-permute-done.6.b3 = f32[4,64,128]{2,1,0:T(8,128)S(1)} collective-permute-done((f32[4,64,128]{2,1,0:T(8,128)S(1)}, f32[4,64,128]{2,1,0:T(8,128)S(1)}, u32[]{:S(2)}, u32[]{:S(2)}) %collective-permute-start.6) | collective-permute-done | bytes 131104 | tf_op jit(solution)/shard_map/ppermute | solution.py:354
  43.4 1.7 %collective-permute-start.7 = (f32[16,32,128]{2,1,0:T(8,128)S(1)}, f32[16,32,128]{2,1,0:T(8,128)S(1)}, u32[]{:S(2)}, u32[]{:S(2)}) collective-permute-start(f32[16,32,128]{2,1,0:T(8,128)S(1)} %all-to-all-done.1.gr), channel_id=1, source_target_pairs={{0,1},{1,0},{2,3},{3,2},{4,5},{5,4},{6,7},{7,6},{8,9},{9,8},{10,11... | collective-permute-start | bytes 786440 | tf_op jit(solution)/shard_map/ppermute | solution.py:350
  46.5 2.4 %shard_map.96 = (f32[8,64,128]{2,1,0:T(8,128)S(1)}, f32[9,64,128]{2,1,0:T(8,128)S(1)}, f32[16,64,128]{2,1,0:T(8,128)}, f32[4,64,128]{2,1,0:T(8,128)S(1)}, f32[4,...) custom-call(s32[3,4]{1,0:T(4,128)S(1)} %copy-done.2, s32[1]{0:T(128)S(6)} %copy.10.counts, s32[1]{0:T(128)} %bitcast.1.code_ref, ...), custom_call_target="tpu_custom_call" | custom-call | tf_op jit(solution)/shard_map/pallas_call | solution.py:47
  49.0 3.9 %all-to-all-start.2 = ((f32[16,64,128]{2,1,0:T(8,128)}), f32[16,64,128]{2,1,0:T(8,128)S(1)}, u32[]{:S(2)}, u32[]{:S(2)}) async-start(f32[16,64,128]{2,1,0:T(8,128)} %get-tuple-element.51), calls=%async_computation.2 | async-start | bytes 1048576 | tf_op jit(solution)/shard_map/all_to_all | solution.py:346
  53.1 1.2 collective-permute-start.10
  54.3 1.6 collective-permute-start.11
  56.0 2.9 %collective-permute-start.9 = (f32[136,128]{1,0:T(8,128)S(1)}, f32[136,128]{1,0:T(8,128)S(1)}, u32[]{:S(2)}, u32[]{:S(2)}) collective-permute-start(f32[136,128]{1,0:T(8,128)S(1)} %get-tuple-element.82), channel_id=1, source_target_pairs={{0,4},{2,6},{4,0},{6,2},{8,12},{10,14},{12,8},{14,10},{1,5},{3,7},... | collective-permute-start | bytes 208904 | tf_op jit(solution)/shard_map/ppermute | solution.py:362
  58.8 1.6 collective-permute-done.10.s2
  60.9 3.2 %collective-permute-start.12 = (f32[160,128]{1,0:T(8,128)S(1)}, f32[160,128]{1,0:T(8,128)S(1)}, u32[]{:S(2)}, u32[]{:S(2)}) collective-permute-start(f32[160,128]{1,0:T(8,128)S(1)} %shard_map.98.mine), channel_id=1, source_target_pairs={{0,2},{2,0},{4,6},{6,4},{8,10},{10,8},{12,14},{14,12},{1,3},{3,1},... | collective-permute-start | bytes 245768 | tf_op jit(solution)/shard_map/ppermute | solution.py:366
  64.1 1.8 %collective-permute-done.12.received = f32[160,128]{1,0:T(8,128)S(1)} collective-permute-done((f32[160,128]{1,0:T(8,128)S(1)}, f32[160,128]{1,0:T(8,128)S(1)}, u32[]{:S(2)}, u32[]{:S(2)}) %collective-permute-start.12) | collective-permute-done | bytes 81952 | tf_op jit(solution)/shard_map/ppermute | solution.py:366
  66.9 5.8 %all-to-all-start.3 = ((f32[16,104,128]{2,1,0:T(8,128)}), f32[16,104,128]{2,1,0:T(8,128)S(1)}, u32[]{:S(2)}, u32[]{:S(2)}) async-start(f32[16,104,128]{2,1,0:T(8,128)} %get-tuple-element.53), calls=%async_computation.3 | async-start | bytes 1703936 | tf_op jit(solution)/shard_map/all_to_all | solution.py:346
  72.8 3.7 %collective-permute-start.13 = (f32[2,64,128]{2,1,0:T(8,128)S(1)}, f32[2,64,128]{2,1,0:T(8,128)S(1)}, u32[]{:S(2)}, u32[]{:S(2)}) collective-permute-start(f32[2,64,128]{2,1,0:T(8,128)S(1)} %get-tuple-element.52.s0), channel_id=1, source_target_pairs={{0,4},{2,6},{4,0},{6,2},{8,12},{10,14},{12,8},{14,10},{1,5},{3,7},... | collective-permute-start | bytes 196616 | tf_op jit(solution)/shard_map/ppermute | solution.py:362
  76.5 1.7 %collective-permute-start.14 = (f32[2,64,128]{2,1,0:T(8,128)S(1)}, f32[2,64,128]{2,1,0:T(8,128)S(1)}, u32[]{:S(2)}, u32[]{:S(2)}) collective-permute-start(f32[2,64,128]{2,1,0:T(8,128)S(1)} %get-tuple-element.52.s0), channel_id=1, source_target_pairs={{0,8},{2,10},{4,12},{6,14},{8,0},{10,2},{12,4},{14,6},{1,9},{3,11}... | collective-permute-start | bytes 196616 | tf_op jit(solution)/shard_map/ppermute | solution.py:362
  78.2 1.7 %collective-permute-start.15 = (f32[2,64,128]{2,1,0:T(8,128)S(1)}, f32[2,64,128]{2,1,0:T(8,128)S(1)}, u32[]{:S(2)}, u32[]{:S(2)}) collective-permute-start(f32[2,64,128]{2,1,0:T(8,128)S(1)} %get-tuple-element.52.s0), channel_id=1, source_target_pairs={{0,12},{2,14},{4,8},{6,10},{8,4},{10,6},{12,0},{14,2},{1,13},{3,15... | collective-permute-start | bytes 196616 | tf_op jit(solution)/shard_map/ppermute | solution.py:362
  79.8 3.9 %collective-permute-done.14.s2 = f32[2,64,128]{2,1,0:T(8,128)S(1)} collective-permute-done((f32[2,64,128]{2,1,0:T(8,128)S(1)}, f32[2,64,128]{2,1,0:T(8,128)S(1)}, u32[]{:S(2)}, u32[]{:S(2)}) %collective-permute-start.14) | collective-permute-done | bytes 65568 | tf_op jit(solution)/shard_map/ppermute | solution.py:362
  83.8 1.4 collective-permute-done.15.s3
  85.2 3.3 %collective-permute-start.16 = (f32[8,64,128]{2,1,0:T(8,128)S(1)}, f32[8,64,128]{2,1,0:T(8,128)S(1)}, u32[]{:S(2)}, u32[]{:S(2)}) collective-permute-start(f32[8,64,128]{2,1,0:T(8,128)S(1)} %shard_map.100.az), channel_id=1, source_target_pairs={{0,1},{1,0},{2,3},{3,2},{4,5},{5,4},{6,7},{7,6},{8,9},{9,8},{10,11... | collective-permute-start | bytes 786440 | tf_op jit(solution)/shard_map/ppermute | solution.py:350
  88.5 1.2 collective-permute-done.16.ao
  89.6 2.9 %shard_map.101 = (f32[8,64,128]{2,1,0:T(8,128)S(1)}, f32[9,64,128]{2,1,0:T(8,128)S(1)}, f32[16,64,128]{2,1,0:T(8,128)}, f32[4,128,128]{2,1,0:T(8,128)S(1)}, f32[...) custom-call(s32[3,4]{1,0:T(4,128)S(1)} %copy-done.2, s32[1]{0:T(128)S(6)} %copy.10.counts, s32[1]{0:T(128)} %bitcast.1.code_ref, ...), custom_call_target="tpu_custom_call" | custom-call | tf_op jit(solution)/shard_map/pallas_call | solution.py:47
  92.9 6.6 %all-to-all-start.4 = ((f32[16,64,128]{2,1,0:T(8,128)}), f32[16,64,128]{2,1,0:T(8,128)S(1)}, u32[]{:S(2)}, u32[]{:S(2)}) async-start(f32[16,64,128]{2,1,0:T(8,128)} %get-tuple-element.61), calls=%async_computation.4 | async-start | bytes 1048576 | tf_op jit(solution)/shard_map/all_to_all | solution.py:346
  99.6 1.4 collective-permute-start.18
  100.9 3.9 %collective-permute-start.19 = (f32[136,128]{1,0:T(8,128)S(1)}, f32[136,128]{1,0:T(8,128)S(1)}, u32[]{:S(2)}, u32[]{:S(2)}) collective-permute-start(f32[136,128]{1,0:T(8,128)S(1)} %get-tuple-element.78), channel_id=1, source_target_pairs={{0,8},{2,10},{4,12},{6,14},{8,0},{10,2},{12,4},{14,6},{1,9},{3,11}... | collective-permute-start | bytes 208904 | tf_op jit(solution)/shard_map/ppermute | solution.py:362
  105.3 3.0 %collective-permute-done.19.s2 = f32[136,128]{1,0:T(8,128)S(1)} collective-permute-done((f32[136,128]{1,0:T(8,128)S(1)}, f32[136,128]{1,0:T(8,128)S(1)}, u32[]{:S(2)}, u32[]{:S(2)}) %collective-permute-start.19) | collective-permute-done | bytes 69664 | tf_op jit(solution)/shard_map/ppermute | solution.py:362
  108.3 2.4 %collective-permute-done.20.s3 = f32[136,128]{1,0:T(8,128)S(1)} collective-permute-done((f32[136,128]{1,0:T(8,128)S(1)}, f32[136,128]{1,0:T(8,128)S(1)}, u32[]{:S(2)}, u32[]{:S(2)}) %collective-permute-start.20) | collective-permute-done | bytes 69664 | tf_op jit(solution)/shard_map/ppermute | solution.py:362
  110.8 3.3 %collective-permute-start.21 = (f32[160,128]{1,0:T(8,128)S(1)}, f32[160,128]{1,0:T(8,128)S(1)}, u32[]{:S(2)}, u32[]{:S(2)}) collective-permute-start(f32[160,128]{1,0:T(8,128)S(1)} %shard_map.103.mine), channel_id=1, source_target_pairs={{0,2},{2,0},{4,6},{6,4},{8,10},{10,8},{12,14},{14,12},{1,3},{3,1},... | collective-permute-start | bytes 245768 | tf_op jit(solution)/shard_map/ppermute | solution.py:366
  114.1 2.3 %collective-permute-done.21.received = f32[160,128]{1,0:T(8,128)S(1)} collective-permute-done((f32[160,128]{1,0:T(8,128)S(1)}, f32[160,128]{1,0:T(8,128)S(1)}, u32[]{:S(2)}, u32[]{:S(2)}) %collective-permute-start.21) | collective-permute-done | bytes 81952 | tf_op jit(solution)/shard_map/ppermute | solution.py:366
  117.4 6.8 %all-to-all-start.5 = ((f32[16,104,128]{2,1,0:T(8,128)}), f32[16,104,128]{2,1,0:T(8,128)S(1)}, u32[]{:S(2)}, u32[]{:S(2)}) async-start(f32[16,104,128]{2,1,0:T(8,128)} %get-tuple-element.63), calls=%async_computation.5 | async-start | bytes 1703936 | tf_op jit(solution)/shard_map/all_to_all | solution.py:346
  124.2 1.6 collective-permute-start.22
  125.8 2.3 %collective-permute-start.23 = (f32[2,64,128]{2,1,0:T(8,128)S(1)}, f32[2,64,128]{2,1,0:T(8,128)S(1)}, u32[]{:S(2)}, u32[]{:S(2)}) collective-permute-start(f32[2,64,128]{2,1,0:T(8,128)S(1)} %get-tuple-element.62.s0), channel_id=1, source_target_pairs={{0,8},{2,10},{4,12},{6,14},{8,0},{10,2},{12,4},{14,6},{1,9},{3,11}... | collective-permute-start | bytes 196616 | tf_op jit(solution)/shard_map/ppermute | solution.py:362
  128.1 1.8 %collective-permute-start.24 = (f32[2,64,128]{2,1,0:T(8,128)S(1)}, f32[2,64,128]{2,1,0:T(8,128)S(1)}, u32[]{:S(2)}, u32[]{:S(2)}) collective-permute-start(f32[2,64,128]{2,1,0:T(8,128)S(1)} %get-tuple-element.62.s0), channel_id=1, source_target_pairs={{0,12},{2,14},{4,8},{6,10},{8,4},{10,6},{12,0},{14,2},{1,13},{3,15... | collective-permute-start | bytes 196616 | tf_op jit(solution)/shard_map/ppermute | solution.py:362
  129.9 3.6 %collective-permute-done.23.s2 = f32[2,64,128]{2,1,0:T(8,128)S(1)} collective-permute-done((f32[2,64,128]{2,1,0:T(8,128)S(1)}, f32[2,64,128]{2,1,0:T(8,128)S(1)}, u32[]{:S(2)}, u32[]{:S(2)}) %collective-permute-start.23) | collective-permute-done | bytes 65568 | tf_op jit(solution)/shard_map/ppermute | solution.py:362
  134.7 3.0 %collective-permute-start.25 = (f32[8,64,128]{2,1,0:T(8,128)S(1)}, f32[8,64,128]{2,1,0:T(8,128)S(1)}, u32[]{:S(2)}, u32[]{:S(2)}) collective-permute-start(f32[8,64,128]{2,1,0:T(8,128)S(1)} %shard_map.105.az), channel_id=1, source_target_pairs={{0,1},{1,0},{2,3},{3,2},{4,5},{5,4},{6,7},{7,6},{8,9},{9,8},{10,11... | collective-permute-start | bytes 786440 | tf_op jit(solution)/shard_map/ppermute | solution.py:350
  137.7 1.2 collective-permute-done.25.ao
  138.8 2.4 %shard_map.106 = (f32[64,128]{1,0:T(8,128)S(1)}, f32[64,128]{1,0:T(8,128)S(1)}, f32[64,128]{1,0:T(8,128)S(1)}, f32[8,128]{1,0:T(8,128)S(1)}, f32[256,1,128]{2,1,0:T(1,128)}) custom-call(s32[3,4]{1,0:T(4,128)S(1)} %copy-done.2, s32[1]{0:T(128)S(6)} %copy.10.counts, s32[1]{0:T(128)} %bitcast.1.code_ref, f32[8,64,128]{2,1,0:T(8,128)S(1)} %shard_map.105.az, ...), custom_call_target="tpu_custom_call" | custom-call | tf_op jit(solution)/shard_map/pallas_call | solution.py:47
  141.2 10.6 %all-to-all-start.6 = ((f32[256,1,128]{2,1,0:T(1,128)}), f32[256,1,128]{2,1,0:T(1,128)S(1)}, u32[]{:S(2)}, u32[]{:S(2)}) async-start(f32[256,1,128]{2,1,0:T(1,128)} %get-tuple-element.69), calls=%async_computation.6 | async-start | bytes 262144 | tf_op jit(solution)/shard_map/all_to_all | solution.py:429
  152.4 12.2 %all-to-all-done.6 = f32[256,1,128]{2,1,0:T(1,128)S(1)} async-done(((f32[256,1,128]{2,1,0:T(1,128)}), f32[256,1,128]{2,1,0:T(1,128)S(1)}, u32[]{:S(2)}, u32[]{:S(2)}) %all-to-all-start.6) | async-done | bytes 131104 | tf_op jit(solution)/shard_map/all_to_all | solution.py:429
  (41 shorter events, 7.9 us)
Async XLA Ops:
  2.2 9.1 %copy-start.1 = (f32[64,128]{1,0:T(8,128)S(1)}, f32[64,128]{1,0:T(8,128)}, u32[]{:S(2)}) copy-start(f32[64,128]{1,0:T(8,128)} %get-tuple-element.41.b0) | copy-start | bytes 98308
  2.2 20.4 %all-to-all-start = ((f32[8,72,128]{2,1,0:T(8,128)}), f32[8,72,128]{2,1,0:T(8,128)S(1)}, u32[]{:S(2)}, u32[]{:S(2)}) async-start(f32[8,72,128]{2,1,0:T(8,128)} %get-tuple-element.40), calls=%async_computation | async-start | bytes 589824 | tf_op jit(solution)/shard_map/all_to_all | solution.py:342
  11.3 3.9 %collective-permute-start.1 = (f32[64,128]{1,0:T(8,128)S(1)}, f32[64,128]{1,0:T(8,128)S(1)}, u32[]{:S(2)}, u32[]{:S(2)}) collective-permute-start(f32[64,128]{1,0:T(8,128)S(1)} %copy-done.1), channel_id=1, source_target_pairs={{0,16},{16,0},{32,48},{48,32},{1,17},{17,1},{33,49},{49,33},{2,18}... | collective-permute-start | bytes 98312 | tf_op jit(solution)/shard_map/ppermute | solution.py:354
  12.6 4.3 %collective-permute-start.2 = (f32[64,128]{1,0:T(8,128)S(1)}, f32[64,128]{1,0:T(8,128)S(1)}, u32[]{:S(2)}, u32[]{:S(2)}) collective-permute-start(f32[64,128]{1,0:T(8,128)S(1)} %copy-done.1), channel_id=1, source_target_pairs={{0,32},{16,48},{32,0},{48,16},{1,33},{17,49},{33,1},{49,17},{2,34}... | collective-permute-start | bytes 98312 | tf_op jit(solution)/shard_map/ppermute | solution.py:354
  15.0 4.3 %collective-permute-start.3 = (f32[64,128]{1,0:T(8,128)S(1)}, f32[64,128]{1,0:T(8,128)S(1)}, u32[]{:S(2)}, u32[]{:S(2)}) collective-permute-start(f32[64,128]{1,0:T(8,128)S(1)} %copy-done.1), channel_id=1, source_target_pairs={{0,48},{16,32},{32,16},{48,0},{1,49},{17,33},{33,17},{49,1},{2,50}... | collective-permute-start | bytes 98312 | tf_op jit(solution)/shard_map/ppermute | solution.py:354
  23.3 22.9 %copy-start = (bf16[4,128,128]{2,1,0:T(8,128)(2,1)S(1)}, bf16[4,128,128]{2,1,0:T(8,128)(2,1)}, u32[]{:S(2)}) copy-start(bf16[4,128,128]{2,1,0:T(8,128)(2,1)} %data.1) | copy-start | bytes 393220
  23.4 20.1 %all-to-all-start.1 = ((f32[16,32,128]{2,1,0:T(8,128)}), f32[16,32,128]{2,1,0:T(8,128)S(1)}, u32[]{:S(2)}, u32[]{:S(2)}) async-start(f32[16,32,128]{2,1,0:T(8,128)} %get-tuple-element.42), calls=%async_computation.1 | async-start | bytes 524288 | tf_op jit(solution)/shard_map/all_to_all | solution.py:346
  30.2 7.3 %collective-permute-start.4 = (f32[4,64,128]{2,1,0:T(8,128)S(1)}, f32[4,64,128]{2,1,0:T(8,128)S(1)}, u32[]{:S(2)}, u32[]{:S(2)}) collective-permute-start(f32[4,64,128]{2,1,0:T(8,128)S(1)} %get-tuple-element.44.b0), channel_id=1, source_target_pairs={{0,64},{64,0},{128,192},{192,128},{1,65},{65,1},{129,193},{193,129... | collective-permute-start | bytes 393224 | tf_op jit(solution)/shard_map/ppermute | solution.py:354
  31.6 9.5 %collective-permute-start.5 = (f32[4,64,128]{2,1,0:T(8,128)S(1)}, f32[4,64,128]{2,1,0:T(8,128)S(1)}, u32[]{:S(2)}, u32[]{:S(2)}) collective-permute-start(f32[4,64,128]{2,1,0:T(8,128)S(1)} %get-tuple-element.44.b0), channel_id=1, source_target_pairs={{0,128},{64,192},{128,0},{192,64},{1,129},{65,193},{129,1},{193,65... | collective-permute-start | bytes 393224 | tf_op jit(solution)/shard_map/ppermute | solution.py:354
  34.0 9.4 %collective-permute-start.6 = (f32[4,64,128]{2,1,0:T(8,128)S(1)}, f32[4,64,128]{2,1,0:T(8,128)S(1)}, u32[]{:S(2)}, u32[]{:S(2)}) collective-permute-start(f32[4,64,128]{2,1,0:T(8,128)S(1)} %get-tuple-element.44.b0), channel_id=1, source_target_pairs={{0,192},{64,128},{128,64},{192,0},{1,193},{65,129},{129,65},{193,1... | collective-permute-start | bytes 393224 | tf_op jit(solution)/shard_map/ppermute | solution.py:354
  34.2 11.6 %collective-permute-start = (f32[8,72,128]{2,1,0:T(8,128)S(1)}, f32[8,72,128]{2,1,0:T(8,128)S(1)}, u32[]{:S(2)}, u32[]{:S(2)}) collective-permute-start(f32[8,72,128]{2,1,0:T(8,128)S(1)} %all-to-all-done.gz), channel_id=1, source_target_pairs={{0,1},{1,0},{2,3},{3,2},{4,5},{5,4},{6,7},{7,6},{8,9},{9,8},{10,11... | collective-permute-start | bytes 884744 | tf_op jit(solution)/shard_map/ppermute | solution.py:350
  43.4 2.8 %collective-permute-start.7 = (f32[16,32,128]{2,1,0:T(8,128)S(1)}, f32[16,32,128]{2,1,0:T(8,128)S(1)}, u32[]{:S(2)}, u32[]{:S(2)}) collective-permute-start(f32[16,32,128]{2,1,0:T(8,128)S(1)} %all-to-all-done.1.gr), channel_id=1, source_target_pairs={{0,1},{1,0},{2,3},{3,2},{4,5},{5,4},{6,7},{7,6},{8,9},{9,8},{10,11... | collective-permute-start | bytes 786440 | tf_op jit(solution)/shard_map/ppermute | solution.py:350
  45.8 0.7 copy-start.2
  48.8 4.2 %collective-permute-start.8 = (f32[9,64,128]{2,1,0:T(8,128)S(1)}, f32[9,64,128]{2,1,0:T(8,128)S(1)}, u32[]{:S(2)}, u32[]{:S(2)}) collective-permute-start(f32[9,64,128]{2,1,0:T(8,128)S(1)} %get-tuple-element.50.send), channel_id=1, source_target_pairs={{0,1},{1,0},{2,3},{3,2},{4,5},{5,4},{6,7},{7,6},{8,9},{9,8},{10,11... | collective-permute-start | bytes 884744 | tf_op jit(solution)/shard_map/ppermute | solution.py:350
  49.0 16.9 %all-to-all-start.2 = ((f32[16,64,128]{2,1,0:T(8,128)}), f32[16,64,128]{2,1,0:T(8,128)S(1)}, u32[]{:S(2)}, u32[]{:S(2)}) async-start(f32[16,64,128]{2,1,0:T(8,128)} %get-tuple-element.51), calls=%async_computation.2 | async-start | bytes 1048576 | tf_op jit(solution)/shard_map/all_to_all | solution.py:346
  53.1 7.3 %collective-permute-start.10 = (f32[136,128]{1,0:T(8,128)S(1)}, f32[136,128]{1,0:T(8,128)S(1)}, u32[]{:S(2)}, u32[]{:S(2)}) collective-permute-start(f32[136,128]{1,0:T(8,128)S(1)} %get-tuple-element.81), channel_id=1, source_target_pairs={{0,8},{2,10},{4,12},{6,14},{8,0},{10,2},{12,4},{14,6},{1,9},{3,11}... | collective-permute-start | bytes 208904 | tf_op jit(solution)/shard_map/ppermute | solution.py:362
  54.3 6.4 %collective-permute-start.11 = (f32[136,128]{1,0:T(8,128)S(1)}, f32[136,128]{1,0:T(8,128)S(1)}, u32[]{:S(2)}, u32[]{:S(2)}) collective-permute-start(f32[136,128]{1,0:T(8,128)S(1)} %get-tuple-element.80), channel_id=1, source_target_pairs={{0,12},{2,14},{4,8},{6,10},{8,4},{10,6},{12,0},{14,2},{1,13},{3,15... | collective-permute-start | bytes 208904 | tf_op jit(solution)/shard_map/ppermute | solution.py:362
  56.0 4.9 %collective-permute-start.9 = (f32[136,128]{1,0:T(8,128)S(1)}, f32[136,128]{1,0:T(8,128)S(1)}, u32[]{:S(2)}, u32[]{:S(2)}) collective-permute-start(f32[136,128]{1,0:T(8,128)S(1)} %get-tuple-element.82), channel_id=1, source_target_pairs={{0,4},{2,6},{4,0},{6,2},{8,12},{10,14},{12,8},{14,10},{1,5},{3,7},... | collective-permute-start | bytes 208904 | tf_op jit(solution)/shard_map/ppermute | solution.py:362
  60.9 5.0 %collective-permute-start.12 = (f32[160,128]{1,0:T(8,128)S(1)}, f32[160,128]{1,0:T(8,128)S(1)}, u32[]{:S(2)}, u32[]{:S(2)}) collective-permute-start(f32[160,128]{1,0:T(8,128)S(1)} %shard_map.98.mine), channel_id=1, source_target_pairs={{0,2},{2,0},{4,6},{6,4},{8,10},{10,8},{12,14},{14,12},{1,3},{3,1},... | collective-permute-start | bytes 245768 | tf_op jit(solution)/shard_map/ppermute | solution.py:366
  66.9 22.7 %all-to-all-start.3 = ((f32[16,104,128]{2,1,0:T(8,128)}), f32[16,104,128]{2,1,0:T(8,128)S(1)}, u32[]{:S(2)}, u32[]{:S(2)}) async-start(f32[16,104,128]{2,1,0:T(8,128)} %get-tuple-element.53), calls=%async_computation.3 | async-start | bytes 1703936 | tf_op jit(solution)/shard_map/all_to_all | solution.py:346
  72.8 7.1 %collective-permute-start.13 = (f32[2,64,128]{2,1,0:T(8,128)S(1)}, f32[2,64,128]{2,1,0:T(8,128)S(1)}, u32[]{:S(2)}, u32[]{:S(2)}) collective-permute-start(f32[2,64,128]{2,1,0:T(8,128)S(1)} %get-tuple-element.52.s0), channel_id=1, source_target_pairs={{0,4},{2,6},{4,0},{6,2},{8,12},{10,14},{12,8},{14,10},{1,5},{3,7},... | collective-permute-start | bytes 196616 | tf_op jit(solution)/shard_map/ppermute | solution.py:362
  76.5 7.3 %collective-permute-start.14 = (f32[2,64,128]{2,1,0:T(8,128)S(1)}, f32[2,64,128]{2,1,0:T(8,128)S(1)}, u32[]{:S(2)}, u32[]{:S(2)}) collective-permute-start(f32[2,64,128]{2,1,0:T(8,128)S(1)} %get-tuple-element.52.s0), channel_id=1, source_target_pairs={{0,8},{2,10},{4,12},{6,14},{8,0},{10,2},{12,4},{14,6},{1,9},{3,11}... | collective-permute-start | bytes 196616 | tf_op jit(solution)/shard_map/ppermute | solution.py:362
  78.2 7.0 %collective-permute-start.15 = (f32[2,64,128]{2,1,0:T(8,128)S(1)}, f32[2,64,128]{2,1,0:T(8,128)S(1)}, u32[]{:S(2)}, u32[]{:S(2)}) collective-permute-start(f32[2,64,128]{2,1,0:T(8,128)S(1)} %get-tuple-element.52.s0), channel_id=1, source_target_pairs={{0,12},{2,14},{4,8},{6,10},{8,4},{10,6},{12,0},{14,2},{1,13},{3,15... | collective-permute-start | bytes 196616 | tf_op jit(solution)/shard_map/ppermute | solution.py:362
  85.2 4.4 %collective-permute-start.16 = (f32[8,64,128]{2,1,0:T(8,128)S(1)}, f32[8,64,128]{2,1,0:T(8,128)S(1)}, u32[]{:S(2)}, u32[]{:S(2)}) collective-permute-start(f32[8,64,128]{2,1,0:T(8,128)S(1)} %shard_map.100.az), channel_id=1, source_target_pairs={{0,1},{1,0},{2,3},{3,2},{4,5},{5,4},{6,7},{7,6},{8,9},{9,8},{10,11... | collective-permute-start | bytes 786440 | tf_op jit(solution)/shard_map/ppermute | solution.py:350
  92.5 7.0 %collective-permute-start.17 = (f32[9,64,128]{2,1,0:T(8,128)S(1)}, f32[9,64,128]{2,1,0:T(8,128)S(1)}, u32[]{:S(2)}, u32[]{:S(2)}) collective-permute-start(f32[9,64,128]{2,1,0:T(8,128)S(1)} %get-tuple-element.60.send), channel_id=1, source_target_pairs={{0,1},{1,0},{2,3},{3,2},{4,5},{5,4},{6,7},{7,6},{8,9},{9,8},{10,11... | collective-permute-start | bytes 884744 | tf_op jit(solution)/shard_map/ppermute | solution.py:350
  92.9 23.5 %all-to-all-start.4 = ((f32[16,64,128]{2,1,0:T(8,128)}), f32[16,64,128]{2,1,0:T(8,128)S(1)}, u32[]{:S(2)}, u32[]{:S(2)}) async-start(f32[16,64,128]{2,1,0:T(8,128)} %get-tuple-element.61), calls=%async_computation.4 | async-start | bytes 1048576 | tf_op jit(solution)/shard_map/all_to_all | solution.py:346
  99.6 5.7 %collective-permute-start.18 = (f32[136,128]{1,0:T(8,128)S(1)}, f32[136,128]{1,0:T(8,128)S(1)}, u32[]{:S(2)}, u32[]{:S(2)}) collective-permute-start(f32[136,128]{1,0:T(8,128)S(1)} %get-tuple-element.79), channel_id=1, source_target_pairs={{0,4},{2,6},{4,0},{6,2},{8,12},{10,14},{12,8},{14,10},{1,5},{3,7},... | collective-permute-start | bytes 208904 | tf_op jit(solution)/shard_map/ppermute | solution.py:362
  100.9 7.4 %collective-permute-start.19 = (f32[136,128]{1,0:T(8,128)S(1)}, f32[136,128]{1,0:T(8,128)S(1)}, u32[]{:S(2)}, u32[]{:S(2)}) collective-permute-start(f32[136,128]{1,0:T(8,128)S(1)} %get-tuple-element.78), channel_id=1, source_target_pairs={{0,8},{2,10},{4,12},{6,14},{8,0},{10,2},{12,4},{14,6},{1,9},{3,11}... | collective-permute-start | bytes 208904 | tf_op jit(solution)/shard_map/ppermute | solution.py:362
  104.8 5.9 %collective-permute-start.20 = (f32[136,128]{1,0:T(8,128)S(1)}, f32[136,128]{1,0:T(8,128)S(1)}, u32[]{:S(2)}, u32[]{:S(2)}) collective-permute-start(f32[136,128]{1,0:T(8,128)S(1)} %get-tuple-element.77), channel_id=1, source_target_pairs={{0,12},{2,14},{4,8},{6,10},{8,4},{10,6},{12,0},{14,2},{1,13},{3,15... | collective-permute-start | bytes 208904 | tf_op jit(solution)/shard_map/ppermute | solution.py:362
  110.8 5.6 %collective-permute-start.21 = (f32[160,128]{1,0:T(8,128)S(1)}, f32[160,128]{1,0:T(8,128)S(1)}, u32[]{:S(2)}, u32[]{:S(2)}) collective-permute-start(f32[160,128]{1,0:T(8,128)S(1)} %shard_map.103.mine), channel_id=1, source_target_pairs={{0,2},{2,0},{4,6},{6,4},{8,10},{10,8},{12,14},{14,12},{1,3},{3,1},... | collective-permute-start | bytes 245768 | tf_op jit(solution)/shard_map/ppermute | solution.py:366
  117.4 21.5 %all-to-all-start.5 = ((f32[16,104,128]{2,1,0:T(8,128)}), f32[16,104,128]{2,1,0:T(8,128)S(1)}, u32[]{:S(2)}, u32[]{:S(2)}) async-start(f32[16,104,128]{2,1,0:T(8,128)} %get-tuple-element.63), calls=%async_computation.5 | async-start | bytes 1703936 | tf_op jit(solution)/shard_map/all_to_all | solution.py:346
  124.2 5.7 %collective-permute-start.22 = (f32[2,64,128]{2,1,0:T(8,128)S(1)}, f32[2,64,128]{2,1,0:T(8,128)S(1)}, u32[]{:S(2)}, u32[]{:S(2)}) collective-permute-start(f32[2,64,128]{2,1,0:T(8,128)S(1)} %get-tuple-element.62.s0), channel_id=1, source_target_pairs={{0,4},{2,6},{4,0},{6,2},{8,12},{10,14},{12,8},{14,10},{1,5},{3,7},... | collective-permute-start | bytes 196616 | tf_op jit(solution)/shard_map/ppermute | solution.py:362
  125.8 7.7 %collective-permute-start.23 = (f32[2,64,128]{2,1,0:T(8,128)S(1)}, f32[2,64,128]{2,1,0:T(8,128)S(1)}, u32[]{:S(2)}, u32[]{:S(2)}) collective-permute-start(f32[2,64,128]{2,1,0:T(8,128)S(1)} %get-tuple-element.62.s0), channel_id=1, source_target_pairs={{0,8},{2,10},{4,12},{6,14},{8,0},{10,2},{12,4},{14,6},{1,9},{3,11}... | collective-permute-start | bytes 196616 | tf_op jit(solution)/shard_map/ppermute | solution.py:362
  128.1 6.5 %collective-permute-start.24 = (f32[2,64,128]{2,1,0:T(8,128)S(1)}, f32[2,64,128]{2,1,0:T(8,128)S(1)}, u32[]{:S(2)}, u32[]{:S(2)}) collective-permute-start(f32[2,64,128]{2,1,0:T(8,128)S(1)} %get-tuple-element.62.s0), channel_id=1, source_target_pairs={{0,12},{2,14},{4,8},{6,10},{8,4},{10,6},{12,0},{14,2},{1,13},{3,15... | collective-permute-start | bytes 196616 | tf_op jit(solution)/shard_map/ppermute | solution.py:362
  134.7 4.1 %collective-permute-start.25 = (f32[8,64,128]{2,1,0:T(8,128)S(1)}, f32[8,64,128]{2,1,0:T(8,128)S(1)}, u32[]{:S(2)}, u32[]{:S(2)}) collective-permute-start(f32[8,64,128]{2,1,0:T(8,128)S(1)} %shard_map.105.az), channel_id=1, source_target_pairs={{0,1},{1,0},{2,3},{3,2},{4,5},{5,4},{6,7},{7,6},{8,9},{9,8},{10,11... | collective-permute-start | bytes 786440 | tf_op jit(solution)/shard_map/ppermute | solution.py:350
  141.2 23.4 %all-to-all-start.6 = ((f32[256,1,128]{2,1,0:T(1,128)}), f32[256,1,128]{2,1,0:T(1,128)S(1)}, u32[]{:S(2)}, u32[]{:S(2)}) async-start(f32[256,1,128]{2,1,0:T(1,128)} %get-tuple-element.69), calls=%async_computation.6 | async-start | bytes 262144 | tf_op jit(solution)/shard_map/all_to_all | solution.py:429

commit v2 on v1

--- a/solution.py
+++ b/solution.py
@@ -197,11 +197,14 @@
         out[2 * R + 8 * k : 2 * R + 8 * k + 8] = part
 
 
-def sum_body(mine, received, gr, ga, gb, couple, out, *, scalars):
+def couple_body(mine, received, ga, couple):
     own = mine[:R] + received[R : 2 * R]
     ga[...] = own
     couple[0] = own
     couple[1] = mine[R : 2 * R] + received[:R]
+
+
+def sum_body(mine, received, gr, gb, out, *, scalars):
     total = gr[0]
     for p in range(1, NP):
         total = total + gr[p]
@@ -377,10 +380,12 @@
         shaped(2 * R + 32, T),
         (joined, *strides),
     )
-    ga, gb, couple, payload = call(
+    received = pair_swap(mine)
+    ga, couple = call(couple_body, (shaped(R, T), shaped(2, R, T)), (mine, received))
+    gb, payload = call(
         functools.partial(sum_body, scalars=scalars),
-        (shaped(R, T), shaped(R, T), shaped(2, R, T), shaped(NP, R + 40, T)),
-        (mine, pair_swap(mine), gr),
+        (shaped(R, T), shaped(NP, R + 40, T)),
+        (mine, received, gr),
     )
     br = along_row(payload)
     line = [couple]

time: 167 us -> 167 us (level)
    pallas_call x14 -> x16, Pallas kernels: 12.9 us -> 13 us  [call(): pl.pallas_call(body, out_shape=outs, in_specs=[SMEM] * scalars + [VMEM] *...]
where the time goes in v2:
time: 167 us; the launch traced here: 166 us
  starting transfers between devices  100 us (60%)
  waiting for transfers between devices  49.9 us (30%)
  Pallas kernels  13 us (8%)
  between operations  2.09 us (1%)
    all_to_all x5, starting transfers between devices, along_row(): return lax.all_to_all(x, ROW, 0, 0, tiled=True)  30.1 us
    ppermute x12, starting transfers between devices, pair_shift(): return lax.ppermute(x, 'z', [(i, i ^ 2 * k) for i in range(8)])  24.3 us
    ppermute x12, waiting for transfers between devices, pair_shift(): return lax.ppermute(x, 'z', [(i, i ^ 2 * k) for i in range(8)])  17.5 us
    pallas_call x16, Pallas kernels, call(): pl.pallas_call(body, out_shape=outs, in_specs=[SMEM] * scalars + [VMEM] *...  13 us
    all_to_all x1, waiting for transfers between devices, step_of(): sums = jnp.sum(lax.all_to_all(spread, ALL, 0, 0, tiled=True), axis=0)  12.2 us
    ppermute x6, starting transfers between devices, swap(): return lax.ppermute(x, 'c', [(0, 1), (1, 0)])  11.9 us
    all_to_all x1, starting transfers between devices, step_of(): sums = jnp.sum(lax.all_to_all(spread, ALL, 0, 0, tiled=True), axis=0)  10.6 us
    ppermute x6, waiting for transfers between devices, shift(): return lax.ppermute(x, axis, [(i, i ^ k) for i in range(4)])  9.93 us
  transfers between devices with their start and end apart: 33, of which 20 were waited for; matrix products, arithmetic and copies ran while one was open for 0% of the time, Pallas kernels for 0%

profile of v2, /device:TPU:1, one launch (start us, length us, event | category | flops | bytes accessed | tf_op | source)
XLA Modules:
  0.0 165.9 jit_solution(6004174628143948950)
XLA Ops:
  0.6 1.5 shard_map.94
  2.2 9.1 %all-to-all-start = ((f32[8,72,128]{2,1,0:T(8,128)}), f32[8,72,128]{2,1,0:T(8,128)S(1)}, u32[]{:S(2)}, u32[]{:S(2)}) async-start(f32[8,72,128]{2,1,0:T(8,128)} %get-tuple-element.40), calls=%async_computation | async-start | bytes 589824 | tf_op jit(solution)/shard_map/all_to_all | solution.py:345
  11.3 1.3 collective-permute-start.1
  12.6 2.5 %collective-permute-start.2 = (f32[64,128]{1,0:T(8,128)S(1)}, f32[64,128]{1,0:T(8,128)S(1)}, u32[]{:S(2)}, u32[]{:S(2)}) collective-permute-start(f32[64,128]{1,0:T(8,128)S(1)} %copy-done.1), channel_id=1, source_target_pairs={{0,32},{16,48},{32,0},{48,16},{1,33},{17,49},{33,1},{49,17},{2,34}... | collective-permute-start | bytes 98312 | tf_op jit(solution)/shard_map/ppermute | solution.py:357
  15.2 1.6 collective-permute-done.2.b2
  16.9 2.5 %collective-permute-done.3.b3 = f32[64,128]{1,0:T(8,128)S(1)} collective-permute-done((f32[64,128]{1,0:T(8,128)S(1)}, f32[64,128]{1,0:T(8,128)S(1)}, u32[]{:S(2)}, u32[]{:S(2)}) %collective-permute-start.3) | collective-permute-done | bytes 32800 | tf_op jit(solution)/shard_map/ppermute | solution.py:357
  19.3 3.2 %all-to-all-done.gz = f32[8,72,128]{2,1,0:T(8,128)S(1)} async-done(((f32[8,72,128]{2,1,0:T(8,128)}), f32[8,72,128]{2,1,0:T(8,128)S(1)}, u32[]{:S(2)}, u32[]{:S(2)}) %all-to-all-start) | async-done | bytes 294944 | tf_op jit(solution)/shard_map/all_to_all | solution.py:345
  23.4 6.9 %all-to-all-start.1 = ((f32[16,32,128]{2,1,0:T(8,128)}), f32[16,32,128]{2,1,0:T(8,128)S(1)}, u32[]{:S(2)}, u32[]{:S(2)}) async-start(f32[16,32,128]{2,1,0:T(8,128)} %get-tuple-element.42), calls=%async_computation.1 | async-start | bytes 524288 | tf_op jit(solution)/shard_map/all_to_all | solution.py:349
  30.2 1.4 collective-permute-start.4
  31.6 2.4 %collective-permute-start.5 = (f32[4,64,128]{2,1,0:T(8,128)S(1)}, f32[4,64,128]{2,1,0:T(8,128)S(1)}, u32[]{:S(2)}, u32[]{:S(2)}) collective-permute-start(f32[4,64,128]{2,1,0:T(8,128)S(1)} %get-tuple-element.44.b0), channel_id=1, source_target_pairs={{0,128},{64,192},{128,0},{192,64},{1,129},{65,193},{129,1},{193,65... | collective-permute-start | bytes 393224 | tf_op jit(solution)/shard_map/ppermute | solution.py:357
  34.2 3.4 %collective-permute-start = (f32[8,72,128]{2,1,0:T(8,128)S(1)}, f32[8,72,128]{2,1,0:T(8,128)S(1)}, u32[]{:S(2)}, u32[]{:S(2)}) collective-permute-start(f32[8,72,128]{2,1,0:T(8,128)S(1)} %all-to-all-done.gz), channel_id=1, source_target_pairs={{0,1},{1,0},{2,3},{3,2},{4,5},{5,4},{6,7},{7,6},{8,9},{9,8},{10,11... | collective-permute-start | bytes 884744 | tf_op jit(solution)/shard_map/ppermute | solution.py:353
  37.6 3.5 %collective-permute-done.5.b2 = f32[4,64,128]{2,1,0:T(8,128)S(1)} collective-permute-done((f32[4,64,128]{2,1,0:T(8,128)S(1)}, f32[4,64,128]{2,1,0:T(8,128)S(1)}, u32[]{:S(2)}, u32[]{:S(2)}) %collective-permute-start.5) | collective-permute-done | bytes 131104 | tf_op jit(solution)/shard_map/ppermute | solution.py:357
  41.1 2.3 %collective-permute-done.6.b3 = f32[4,64,128]{2,1,0:T(8,128)S(1)} collective-permute-done((f32[4,64,128]{2,1,0:T(8,128)S(1)}, f32[4,64,128]{2,1,0:T(8,128)S(1)}, u32[]{:S(2)}, u32[]{:S(2)}) %collective-permute-start.6) | collective-permute-done | bytes 131104 | tf_op jit(solution)/shard_map/ppermute | solution.py:357
  43.4 1.7 %collective-permute-start.7 = (f32[16,32,128]{2,1,0:T(8,128)S(1)}, f32[16,32,128]{2,1,0:T(8,128)S(1)}, u32[]{:S(2)}, u32[]{:S(2)}) collective-permute-start(f32[16,32,128]{2,1,0:T(8,128)S(1)} %all-to-all-done.1.gr), channel_id=1, source_target_pairs={{0,1},{1,0},{2,3},{3,2},{4,5},{5,4},{6,7},{7,6},{8,9},{9,8},{10,11... | collective-permute-start | bytes 786440 | tf_op jit(solution)/shard_map/ppermute | solution.py:353
  46.5 2.4 %shard_map.96 = (f32[8,64,128]{2,1,0:T(8,128)S(1)}, f32[9,64,128]{2,1,0:T(8,128)S(1)}, f32[16,64,128]{2,1,0:T(8,128)}, f32[4,64,128]{2,1,0:T(8,128)S(1)}, f32[4,...) custom-call(s32[3,4]{1,0:T(4,128)S(1)} %copy-done.2, s32[1]{0:T(128)S(6)} %copy.10.counts, s32[1]{0:T(128)} %bitcast.1.code_ref, ...), custom_call_target="tpu_custom_call" | custom-call | tf_op jit(solution)/shard_map/pallas_call | solution.py:47
  49.0 3.9 %all-to-all-start.2 = ((f32[16,64,128]{2,1,0:T(8,128)}), f32[16,64,128]{2,1,0:T(8,128)S(1)}, u32[]{:S(2)}, u32[]{:S(2)}) async-start(f32[16,64,128]{2,1,0:T(8,128)} %get-tuple-element.52), calls=%async_computation.2 | async-start | bytes 1048576 | tf_op jit(solution)/shard_map/all_to_all | solution.py:349
  53.1 1.2 collective-permute-start.10
  54.3 1.6 collective-permute-start.11
  55.9 2.9 %collective-permute-start.9 = (f32[136,128]{1,0:T(8,128)S(1)}, f32[136,128]{1,0:T(8,128)S(1)}, u32[]{:S(2)}, u32[]{:S(2)}) collective-permute-start(f32[136,128]{1,0:T(8,128)S(1)} %get-tuple-element.82), channel_id=1, source_target_pairs={{0,4},{2,6},{4,0},{6,2},{8,12},{10,14},{12,8},{14,10},{1,5},{3,7},... | collective-permute-start | bytes 208904 | tf_op jit(solution)/shard_map/ppermute | solution.py:365
  58.8 1.6 collective-permute-done.10.s2
  60.9 3.2 %collective-permute-start.12 = (f32[160,128]{1,0:T(8,128)S(1)}, f32[160,128]{1,0:T(8,128)S(1)}, u32[]{:S(2)}, u32[]{:S(2)}) collective-permute-start(f32[160,128]{1,0:T(8,128)S(1)} %shard_map.98.mine), channel_id=1, source_target_pairs={{0,2},{2,0},{4,6},{6,4},{8,10},{10,8},{12,14},{14,12},{1,3},{3,1},... | collective-permute-start | bytes 245768 | tf_op jit(solution)/shard_map/ppermute | solution.py:369
  64.1 1.8 %collective-permute-done.12.received = f32[160,128]{1,0:T(8,128)S(1)} collective-permute-done((f32[160,128]{1,0:T(8,128)S(1)}, f32[160,128]{1,0:T(8,128)S(1)}, u32[]{:S(2)}, u32[]{:S(2)}) %collective-permute-start.12) | collective-permute-done | bytes 81952 | tf_op jit(solution)/shard_map/ppermute | solution.py:369
  66.9 5.9 %all-to-all-start.3 = ((f32[16,104,128]{2,1,0:T(8,128)}), f32[16,104,128]{2,1,0:T(8,128)S(1)}, u32[]{:S(2)}, u32[]{:S(2)}) async-start(f32[16,104,128]{2,1,0:T(8,128)} %get-tuple-element.53), calls=%async_computation.3 | async-start | bytes 1703936 | tf_op jit(solution)/shard_map/all_to_all | solution.py:349
  72.8 3.7 %collective-permute-start.13 = (f32[2,64,128]{2,1,0:T(8,128)S(1)}, f32[2,64,128]{2,1,0:T(8,128)S(1)}, u32[]{:S(2)}, u32[]{:S(2)}) collective-permute-start(f32[2,64,128]{2,1,0:T(8,128)S(1)} %get-tuple-element.51.s0), channel_id=1, source_target_pairs={{0,4},{2,6},{4,0},{6,2},{8,12},{10,14},{12,8},{14,10},{1,5},{3,7},... | collective-permute-start | bytes 196616 | tf_op jit(solution)/shard_map/ppermute | solution.py:365
  76.5 1.7 %collective-permute-start.14 = (f32[2,64,128]{2,1,0:T(8,128)S(1)}, f32[2,64,128]{2,1,0:T(8,128)S(1)}, u32[]{:S(2)}, u32[]{:S(2)}) collective-permute-start(f32[2,64,128]{2,1,0:T(8,128)S(1)} %get-tuple-element.51.s0), channel_id=1, source_target_pairs={{0,8},{2,10},{4,12},{6,14},{8,0},{10,2},{12,4},{14,6},{1,9},{3,11}... | collective-permute-start | bytes 196616 | tf_op jit(solution)/shard_map/ppermute | solution.py:365
  78.2 1.7 %collective-permute-start.15 = (f32[2,64,128]{2,1,0:T(8,128)S(1)}, f32[2,64,128]{2,1,0:T(8,128)S(1)}, u32[]{:S(2)}, u32[]{:S(2)}) collective-permute-start(f32[2,64,128]{2,1,0:T(8,128)S(1)} %get-tuple-element.51.s0), channel_id=1, source_target_pairs={{0,12},{2,14},{4,8},{6,10},{8,4},{10,6},{12,0},{14,2},{1,13},{3,15... | collective-permute-start | bytes 196616 | tf_op jit(solution)/shard_map/ppermute | solution.py:365
  79.9 3.9 %collective-permute-done.14.s2 = f32[2,64,128]{2,1,0:T(8,128)S(1)} collective-permute-done((f32[2,64,128]{2,1,0:T(8,128)S(1)}, f32[2,64,128]{2,1,0:T(8,128)S(1)}, u32[]{:S(2)}, u32[]{:S(2)}) %collective-permute-start.14) | collective-permute-done | bytes 65568 | tf_op jit(solution)/shard_map/ppermute | solution.py:365
  83.8 1.4 collective-permute-done.15.s3
  85.2 3.3 %collective-permute-start.16 = (f32[8,64,128]{2,1,0:T(8,128)S(1)}, f32[8,64,128]{2,1,0:T(8,128)S(1)}, u32[]{:S(2)}, u32[]{:S(2)}) collective-permute-start(f32[8,64,128]{2,1,0:T(8,128)S(1)} %shard_map.100.az), channel_id=1, source_target_pairs={{0,1},{1,0},{2,3},{3,2},{4,5},{5,4},{6,7},{7,6},{8,9},{9,8},{10,11... | collective-permute-start | bytes 786440 | tf_op jit(solution)/shard_map/ppermute | solution.py:353
  88.5 1.2 collective-permute-done.16.ao
  89.6 2.9 %shard_map.102 = (f32[8,64,128]{2,1,0:T(8,128)S(1)}, f32[9,64,128]{2,1,0:T(8,128)S(1)}, f32[16,64,128]{2,1,0:T(8,128)}, f32[4,128,128]{2,1,0:T(8,128)S(1)}, f32[...) custom-call(s32[3,4]{1,0:T(4,128)S(1)} %copy-done.2, s32[1]{0:T(128)S(6)} %copy.10.counts, s32[1]{0:T(128)} %bitcast.1.code_ref, ...), custom_call_target="tpu_custom_call" | custom-call | tf_op jit(solution)/shard_map/pallas_call | solution.py:47
  92.9 6.7 %all-to-all-start.4 = ((f32[16,64,128]{2,1,0:T(8,128)}), f32[16,64,128]{2,1,0:T(8,128)S(1)}, u32[]{:S(2)}, u32[]{:S(2)}) async-start(f32[16,64,128]{2,1,0:T(8,128)} %get-tuple-element.62), calls=%async_computation.4 | async-start | bytes 1048576 | tf_op jit(solution)/shard_map/all_to_all | solution.py:349
  99.7 1.4 collective-permute-start.18
  101.0 3.9 %collective-permute-start.19 = (f32[136,128]{1,0:T(8,128)S(1)}, f32[136,128]{1,0:T(8,128)S(1)}, u32[]{:S(2)}, u32[]{:S(2)}) collective-permute-start(f32[136,128]{1,0:T(8,128)S(1)} %get-tuple-element.78), channel_id=1, source_target_pairs={{0,8},{2,10},{4,12},{6,14},{8,0},{10,2},{12,4},{14,6},{1,9},{3,11}... | collective-permute-start | bytes 208904 | tf_op jit(solution)/shard_map/ppermute | solution.py:365
  105.4 3.0 %collective-permute-done.19.s2 = f32[136,128]{1,0:T(8,128)S(1)} collective-permute-done((f32[136,128]{1,0:T(8,128)S(1)}, f32[136,128]{1,0:T(8,128)S(1)}, u32[]{:S(2)}, u32[]{:S(2)}) %collective-permute-start.19) | collective-permute-done | bytes 69664 | tf_op jit(solution)/shard_map/ppermute | solution.py:365
  108.4 2.5 %collective-permute-done.20.s3 = f32[136,128]{1,0:T(8,128)S(1)} collective-permute-done((f32[136,128]{1,0:T(8,128)S(1)}, f32[136,128]{1,0:T(8,128)S(1)}, u32[]{:S(2)}, u32[]{:S(2)}) %collective-permute-start.20) | collective-permute-done | bytes 69664 | tf_op jit(solution)/shard_map/ppermute | solution.py:365
  110.9 3.3 %collective-permute-start.21 = (f32[160,128]{1,0:T(8,128)S(1)}, f32[160,128]{1,0:T(8,128)S(1)}, u32[]{:S(2)}, u32[]{:S(2)}) collective-permute-start(f32[160,128]{1,0:T(8,128)S(1)} %shard_map.104.mine), channel_id=1, source_target_pairs={{0,2},{2,0},{4,6},{6,4},{8,10},{10,8},{12,14},{14,12},{1,3},{3,1},... | collective-permute-start | bytes 245768 | tf_op jit(solution)/shard_map/ppermute | solution.py:369
  114.2 2.3 %collective-permute-done.21.received = f32[160,128]{1,0:T(8,128)S(1)} collective-permute-done((f32[160,128]{1,0:T(8,128)S(1)}, f32[160,128]{1,0:T(8,128)S(1)}, u32[]{:S(2)}, u32[]{:S(2)}) %collective-permute-start.21) | collective-permute-done | bytes 81952 | tf_op jit(solution)/shard_map/ppermute | solution.py:369
  117.5 6.8 %all-to-all-start.5 = ((f32[16,104,128]{2,1,0:T(8,128)}), f32[16,104,128]{2,1,0:T(8,128)S(1)}, u32[]{:S(2)}, u32[]{:S(2)}) async-start(f32[16,104,128]{2,1,0:T(8,128)} %get-tuple-element.63), calls=%async_computation.5 | async-start | bytes 1703936 | tf_op jit(solution)/shard_map/all_to_all | solution.py:349
  124.3 1.6 collective-permute-start.22
  125.9 2.3 %collective-permute-start.23 = (f32[2,64,128]{2,1,0:T(8,128)S(1)}, f32[2,64,128]{2,1,0:T(8,128)S(1)}, u32[]{:S(2)}, u32[]{:S(2)}) collective-permute-start(f32[2,64,128]{2,1,0:T(8,128)S(1)} %get-tuple-element.61.s0), channel_id=1, source_target_pairs={{0,8},{2,10},{4,12},{6,14},{8,0},{10,2},{12,4},{14,6},{1,9},{3,11}... | collective-permute-start | bytes 196616 | tf_op jit(solution)/shard_map/ppermute | solution.py:365
  128.3 1.8 %collective-permute-start.24 = (f32[2,64,128]{2,1,0:T(8,128)S(1)}, f32[2,64,128]{2,1,0:T(8,128)S(1)}, u32[]{:S(2)}, u32[]{:S(2)}) collective-permute-start(f32[2,64,128]{2,1,0:T(8,128)S(1)} %get-tuple-element.61.s0), channel_id=1, source_target_pairs={{0,12},{2,14},{4,8},{6,10},{8,4},{10,6},{12,0},{14,2},{1,13},{3,15... | collective-permute-start | bytes 196616 | tf_op jit(solution)/shard_map/ppermute | solution.py:365
  130.0 3.6 %collective-permute-done.23.s2 = f32[2,64,128]{2,1,0:T(8,128)S(1)} collective-permute-done((f32[2,64,128]{2,1,0:T(8,128)S(1)}, f32[2,64,128]{2,1,0:T(8,128)S(1)}, u32[]{:S(2)}, u32[]{:S(2)}) %collective-permute-start.23) | collective-permute-done | bytes 65568 | tf_op jit(solution)/shard_map/ppermute | solution.py:365
  134.8 2.9 %collective-permute-start.25 = (f32[8,64,128]{2,1,0:T(8,128)S(1)}, f32[8,64,128]{2,1,0:T(8,128)S(1)}, u32[]{:S(2)}, u32[]{:S(2)}) collective-permute-start(f32[8,64,128]{2,1,0:T(8,128)S(1)} %shard_map.106.az), channel_id=1, source_target_pairs={{0,1},{1,0},{2,3},{3,2},{4,5},{5,4},{6,7},{7,6},{8,9},{9,8},{10,11... | collective-permute-start | bytes 786440 | tf_op jit(solution)/shard_map/ppermute | solution.py:353
  137.8 1.2 collective-permute-done.25.ao
  138.9 2.4 %shard_map.108 = (f32[64,128]{1,0:T(8,128)S(1)}, f32[64,128]{1,0:T(8,128)S(1)}, f32[64,128]{1,0:T(8,128)S(1)}, f32[8,128]{1,0:T(8,128)S(1)}, f32[256,1,128]{2,1,0:T(1,128)}) custom-call(s32[3,4]{1,0:T(4,128)S(1)} %copy-done.2, s32[1]{0:T(128)S(6)} %copy.10.counts, s32[1]{0:T(128)} %bitcast.1.code_ref, f32[8,64,128]{2,1,0:T(8,128)S(1)} %shard_map.106.az, ...), custom_call_target="tpu_custom_call" | custom-call | tf_op jit(solution)/shard_map/pallas_call | solution.py:47
  141.3 10.6 %all-to-all-start.6 = ((f32[256,1,128]{2,1,0:T(1,128)}), f32[256,1,128]{2,1,0:T(1,128)S(1)}, u32[]{:S(2)}, u32[]{:S(2)}) async-start(f32[256,1,128]{2,1,0:T(1,128)} %get-tuple-element.69), calls=%async_computation.6 | async-start | bytes 262144 | tf_op jit(solution)/shard_map/all_to_all | solution.py:434
  152.6 12.2 %all-to-all-done.6 = f32[256,1,128]{2,1,0:T(1,128)S(1)} async-done(((f32[256,1,128]{2,1,0:T(1,128)}), f32[256,1,128]{2,1,0:T(1,128)S(1)}, u32[]{:S(2)}, u32[]{:S(2)}) %all-to-all-start.6) | async-done | bytes 131104 | tf_op jit(solution)/shard_map/all_to_all | solution.py:434
  (43 shorter events, 7.9 us)
Async XLA Ops:
  2.2 9.1 %copy-start.1 = (f32[64,128]{1,0:T(8,128)S(1)}, f32[64,128]{1,0:T(8,128)}, u32[]{:S(2)}) copy-start(f32[64,128]{1,0:T(8,128)} %get-tuple-element.41.b0) | copy-start | bytes 98308
  2.2 20.4 %all-to-all-start = ((f32[8,72,128]{2,1,0:T(8,128)}), f32[8,72,128]{2,1,0:T(8,128)S(1)}, u32[]{:S(2)}, u32[]{:S(2)}) async-start(f32[8,72,128]{2,1,0:T(8,128)} %get-tuple-element.40), calls=%async_computation | async-start | bytes 589824 | tf_op jit(solution)/shard_map/all_to_all | solution.py:345
  11.3 3.9 %collective-permute-start.1 = (f32[64,128]{1,0:T(8,128)S(1)}, f32[64,128]{1,0:T(8,128)S(1)}, u32[]{:S(2)}, u32[]{:S(2)}) collective-permute-start(f32[64,128]{1,0:T(8,128)S(1)} %copy-done.1), channel_id=1, source_target_pairs={{0,16},{16,0},{32,48},{48,32},{1,17},{17,1},{33,49},{49,33},{2,18}... | collective-permute-start | bytes 98312 | tf_op jit(solution)/shard_map/ppermute | solution.py:357
  12.6 4.3 %collective-permute-start.2 = (f32[64,128]{1,0:T(8,128)S(1)}, f32[64,128]{1,0:T(8,128)S(1)}, u32[]{:S(2)}, u32[]{:S(2)}) collective-permute-start(f32[64,128]{1,0:T(8,128)S(1)} %copy-done.1), channel_id=1, source_target_pairs={{0,32},{16,48},{32,0},{48,16},{1,33},{17,49},{33,1},{49,17},{2,34}... | collective-permute-start | bytes 98312 | tf_op jit(solution)/shard_map/ppermute | solution.py:357
  15.0 4.3 %collective-permute-start.3 = (f32[64,128]{1,0:T(8,128)S(1)}, f32[64,128]{1,0:T(8,128)S(1)}, u32[]{:S(2)}, u32[]{:S(2)}) collective-permute-start(f32[64,128]{1,0:T(8,128)S(1)} %copy-done.1), channel_id=1, source_target_pairs={{0,48},{16,32},{32,16},{48,0},{1,49},{17,33},{33,17},{49,1},{2,50}... | collective-permute-start | bytes 98312 | tf_op jit(solution)/shard_map/ppermute | solution.py:357
  23.3 22.9 %copy-start = (bf16[4,128,128]{2,1,0:T(8,128)(2,1)S(1)}, bf16[4,128,128]{2,1,0:T(8,128)(2,1)}, u32[]{:S(2)}) copy-start(bf16[4,128,128]{2,1,0:T(8,128)(2,1)} %data.1) | copy-start | bytes 393220
  23.4 20.1 %all-to-all-start.1 = ((f32[16,32,128]{2,1,0:T(8,128)}), f32[16,32,128]{2,1,0:T(8,128)S(1)}, u32[]{:S(2)}, u32[]{:S(2)}) async-start(f32[16,32,128]{2,1,0:T(8,128)} %get-tuple-element.42), calls=%async_computation.1 | async-start | bytes 524288 | tf_op jit(solution)/shard_map/all_to_all | solution.py:349
  30.2 7.3 %collective-permute-start.4 = (f32[4,64,128]{2,1,0:T(8,128)S(1)}, f32[4,64,128]{2,1,0:T(8,128)S(1)}, u32[]{:S(2)}, u32[]{:S(2)}) collective-permute-start(f32[4,64,128]{2,1,0:T(8,128)S(1)} %get-tuple-element.44.b0), channel_id=1, source_target_pairs={{0,64},{64,0},{128,192},{192,128},{1,65},{65,1},{129,193},{193,129... | collective-permute-start | bytes 393224 | tf_op jit(solution)/shard_map/ppermute | solution.py:357
  31.6 9.5 %collective-permute-start.5 = (f32[4,64,128]{2,1,0:T(8,128)S(1)}, f32[4,64,128]{2,1,0:T(8,128)S(1)}, u32[]{:S(2)}, u32[]{:S(2)}) collective-permute-start(f32[4,64,128]{2,1,0:T(8,128)S(1)} %get-tuple-element.44.b0), channel_id=1, source_target_pairs={{0,128},{64,192},{128,0},{192,64},{1,129},{65,193},{129,1},{193,65... | collective-permute-start | bytes 393224 | tf_op jit(solution)/shard_map/ppermute | solution.py:357
  34.0 9.4 %collective-permute-start.6 = (f32[4,64,128]{2,1,0:T(8,128)S(1)}, f32[4,64,128]{2,1,0:T(8,128)S(1)}, u32[]{:S(2)}, u32[]{:S(2)}) collective-permute-start(f32[4,64,128]{2,1,0:T(8,128)S(1)} %get-tuple-element.44.b0), channel_id=1, source_target_pairs={{0,192},{64,128},{128,64},{192,0},{1,193},{65,129},{129,65},{193,1... | collective-permute-start | bytes 393224 | tf_op jit(solution)/shard_map/ppermute | solution.py:357
  34.2 11.6 %collective-permute-start = (f32[8,72,128]{2,1,0:T(8,128)S(1)}, f32[8,72,128]{2,1,0:T(8,128)S(1)}, u32[]{:S(2)}, u32[]{:S(2)}) collective-permute-start(f32[8,72,128]{2,1,0:T(8,128)S(1)} %all-to-all-done.gz), channel_id=1, source_target_pairs={{0,1},{1,0},{2,3},{3,2},{4,5},{5,4},{6,7},{7,6},{8,9},{9,8},{10,11... | collective-permute-start | bytes 884744 | tf_op jit(solution)/shard_map/ppermute | solution.py:353
  43.4 2.8 %collective-permute-start.7 = (f32[16,32,128]{2,1,0:T(8,128)S(1)}, f32[16,32,128]{2,1,0:T(8,128)S(1)}, u32[]{:S(2)}, u32[]{:S(2)}) collective-permute-start(f32[16,32,128]{2,1,0:T(8,128)S(1)} %all-to-all-done.1.gr), channel_id=1, source_target_pairs={{0,1},{1,0},{2,3},{3,2},{4,5},{5,4},{6,7},{7,6},{8,9},{9,8},{10,11... | collective-permute-start | bytes 786440 | tf_op jit(solution)/shard_map/ppermute | solution.py:353
  45.8 0.7 copy-start.2
  48.8 4.2 %collective-permute-start.8 = (f32[9,64,128]{2,1,0:T(8,128)S(1)}, f32[9,64,128]{2,1,0:T(8,128)S(1)}, u32[]{:S(2)}, u32[]{:S(2)}) collective-permute-start(f32[9,64,128]{2,1,0:T(8,128)S(1)} %get-tuple-element.50.send), channel_id=1, source_target_pairs={{0,1},{1,0},{2,3},{3,2},{4,5},{5,4},{6,7},{7,6},{8,9},{9,8},{10,11... | collective-permute-start | bytes 884744 | tf_op jit(solution)/shard_map/ppermute | solution.py:353
  49.0 16.9 %all-to-all-start.2 = ((f32[16,64,128]{2,1,0:T(8,128)}), f32[16,64,128]{2,1,0:T(8,128)S(1)}, u32[]{:S(2)}, u32[]{:S(2)}) async-start(f32[16,64,128]{2,1,0:T(8,128)} %get-tuple-element.52), calls=%async_computation.2 | async-start | bytes 1048576 | tf_op jit(solution)/shard_map/all_to_all | solution.py:349
  53.1 7.3 %collective-permute-start.10 = (f32[136,128]{1,0:T(8,128)S(1)}, f32[136,128]{1,0:T(8,128)S(1)}, u32[]{:S(2)}, u32[]{:S(2)}) collective-permute-start(f32[136,128]{1,0:T(8,128)S(1)} %get-tuple-element.81), channel_id=1, source_target_pairs={{0,8},{2,10},{4,12},{6,14},{8,0},{10,2},{12,4},{14,6},{1,9},{3,11}... | collective-permute-start | bytes 208904 | tf_op jit(solution)/shard_map/ppermute | solution.py:365
  54.3 6.4 %collective-permute-start.11 = (f32[136,128]{1,0:T(8,128)S(1)}, f32[136,128]{1,0:T(8,128)S(1)}, u32[]{:S(2)}, u32[]{:S(2)}) collective-permute-start(f32[136,128]{1,0:T(8,128)S(1)} %get-tuple-element.80), channel_id=1, source_target_pairs={{0,12},{2,14},{4,8},{6,10},{8,4},{10,6},{12,0},{14,2},{1,13},{3,15... | collective-permute-start | bytes 208904 | tf_op jit(solution)/shard_map/ppermute | solution.py:365
  55.9 4.9 %collective-permute-start.9 = (f32[136,128]{1,0:T(8,128)S(1)}, f32[136,128]{1,0:T(8,128)S(1)}, u32[]{:S(2)}, u32[]{:S(2)}) collective-permute-start(f32[136,128]{1,0:T(8,128)S(1)} %get-tuple-element.82), channel_id=1, source_target_pairs={{0,4},{2,6},{4,0},{6,2},{8,12},{10,14},{12,8},{14,10},{1,5},{3,7},... | collective-permute-start | bytes 208904 | tf_op jit(solution)/shard_map/ppermute | solution.py:365
  60.9 5.0 %collective-permute-start.12 = (f32[160,128]{1,0:T(8,128)S(1)}, f32[160,128]{1,0:T(8,128)S(1)}, u32[]{:S(2)}, u32[]{:S(2)}) collective-permute-start(f32[160,128]{1,0:T(8,128)S(1)} %shard_map.98.mine), channel_id=1, source_target_pairs={{0,2},{2,0},{4,6},{6,4},{8,10},{10,8},{12,14},{14,12},{1,3},{3,1},... | collective-permute-start | bytes 245768 | tf_op jit(solution)/shard_map/ppermute | solution.py:369
  66.9 22.7 %all-to-all-start.3 = ((f32[16,104,128]{2,1,0:T(8,128)}), f32[16,104,128]{2,1,0:T(8,128)S(1)}, u32[]{:S(2)}, u32[]{:S(2)}) async-start(f32[16,104,128]{2,1,0:T(8,128)} %get-tuple-element.53), calls=%async_computation.3 | async-start | bytes 1703936 | tf_op jit(solution)/shard_map/all_to_all | solution.py:349
  72.8 7.1 %collective-permute-start.13 = (f32[2,64,128]{2,1,0:T(8,128)S(1)}, f32[2,64,128]{2,1,0:T(8,128)S(1)}, u32[]{:S(2)}, u32[]{:S(2)}) collective-permute-start(f32[2,64,128]{2,1,0:T(8,128)S(1)} %get-tuple-element.51.s0), channel_id=1, source_target_pairs={{0,4},{2,6},{4,0},{6,2},{8,12},{10,14},{12,8},{14,10},{1,5},{3,7},... | collective-permute-start | bytes 196616 | tf_op jit(solution)/shard_map/ppermute | solution.py:365
  76.5 7.3 %collective-permute-start.14 = (f32[2,64,128]{2,1,0:T(8,128)S(1)}, f32[2,64,128]{2,1,0:T(8,128)S(1)}, u32[]{:S(2)}, u32[]{:S(2)}) collective-permute-start(f32[2,64,128]{2,1,0:T(8,128)S(1)} %get-tuple-element.51.s0), channel_id=1, source_target_pairs={{0,8},{2,10},{4,12},{6,14},{8,0},{10,2},{12,4},{14,6},{1,9},{3,11}... | collective-permute-start | bytes 196616 | tf_op jit(solution)/shard_map/ppermute | solution.py:365
  78.2 7.0 %collective-permute-start.15 = (f32[2,64,128]{2,1,0:T(8,128)S(1)}, f32[2,64,128]{2,1,0:T(8,128)S(1)}, u32[]{:S(2)}, u32[]{:S(2)}) collective-permute-start(f32[2,64,128]{2,1,0:T(8,128)S(1)} %get-tuple-element.51.s0), channel_id=1, source_target_pairs={{0,12},{2,14},{4,8},{6,10},{8,4},{10,6},{12,0},{14,2},{1,13},{3,15... | collective-permute-start | bytes 196616 | tf_op jit(solution)/shard_map/ppermute | solution.py:365
  85.2 4.4 %collective-permute-start.16 = (f32[8,64,128]{2,1,0:T(8,128)S(1)}, f32[8,64,128]{2,1,0:T(8,128)S(1)}, u32[]{:S(2)}, u32[]{:S(2)}) collective-permute-start(f32[8,64,128]{2,1,0:T(8,128)S(1)} %shard_map.100.az), channel_id=1, source_target_pairs={{0,1},{1,0},{2,3},{3,2},{4,5},{5,4},{6,7},{7,6},{8,9},{9,8},{10,11... | collective-permute-start | bytes 786440 | tf_op jit(solution)/shard_map/ppermute | solution.py:353
  92.5 7.0 %collective-permute-start.17 = (f32[9,64,128]{2,1,0:T(8,128)S(1)}, f32[9,64,128]{2,1,0:T(8,128)S(1)}, u32[]{:S(2)}, u32[]{:S(2)}) collective-permute-start(f32[9,64,128]{2,1,0:T(8,128)S(1)} %get-tuple-element.60.send), channel_id=1, source_target_pairs={{0,1},{1,0},{2,3},{3,2},{4,5},{5,4},{6,7},{7,6},{8,9},{9,8},{10,11... | collective-permute-start | bytes 884744 | tf_op jit(solution)/shard_map/ppermute | solution.py:353
  92.9 23.6 %all-to-all-start.4 = ((f32[16,64,128]{2,1,0:T(8,128)}), f32[16,64,128]{2,1,0:T(8,128)S(1)}, u32[]{:S(2)}, u32[]{:S(2)}) async-start(f32[16,64,128]{2,1,0:T(8,128)} %get-tuple-element.62), calls=%async_computation.4 | async-start | bytes 1048576 | tf_op jit(solution)/shard_map/all_to_all | solution.py:349
  99.7 5.7 %collective-permute-start.18 = (f32[136,128]{1,0:T(8,128)S(1)}, f32[136,128]{1,0:T(8,128)S(1)}, u32[]{:S(2)}, u32[]{:S(2)}) collective-permute-start(f32[136,128]{1,0:T(8,128)S(1)} %get-tuple-element.79), channel_id=1, source_target_pairs={{0,4},{2,6},{4,0},{6,2},{8,12},{10,14},{12,8},{14,10},{1,5},{3,7},... | collective-permute-start | bytes 208904 | tf_op jit(solution)/shard_map/ppermute | solution.py:365
  101.0 7.4 %collective-permute-start.19 = (f32[136,128]{1,0:T(8,128)S(1)}, f32[136,128]{1,0:T(8,128)S(1)}, u32[]{:S(2)}, u32[]{:S(2)}) collective-permute-start(f32[136,128]{1,0:T(8,128)S(1)} %get-tuple-element.78), channel_id=1, source_target_pairs={{0,8},{2,10},{4,12},{6,14},{8,0},{10,2},{12,4},{14,6},{1,9},{3,11}... | collective-permute-start | bytes 208904 | tf_op jit(solution)/shard_map/ppermute | solution.py:365
  104.9 5.9 %collective-permute-start.20 = (f32[136,128]{1,0:T(8,128)S(1)}, f32[136,128]{1,0:T(8,128)S(1)}, u32[]{:S(2)}, u32[]{:S(2)}) collective-permute-start(f32[136,128]{1,0:T(8,128)S(1)} %get-tuple-element.77), channel_id=1, source_target_pairs={{0,12},{2,14},{4,8},{6,10},{8,4},{10,6},{12,0},{14,2},{1,13},{3,15... | collective-permute-start | bytes 208904 | tf_op jit(solution)/shard_map/ppermute | solution.py:365
  110.9 5.6 %collective-permute-start.21 = (f32[160,128]{1,0:T(8,128)S(1)}, f32[160,128]{1,0:T(8,128)S(1)}, u32[]{:S(2)}, u32[]{:S(2)}) collective-permute-start(f32[160,128]{1,0:T(8,128)S(1)} %shard_map.104.mine), channel_id=1, source_target_pairs={{0,2},{2,0},{4,6},{6,4},{8,10},{10,8},{12,14},{14,12},{1,3},{3,1},... | collective-permute-start | bytes 245768 | tf_op jit(solution)/shard_map/ppermute | solution.py:369
  117.5 21.5 %all-to-all-start.5 = ((f32[16,104,128]{2,1,0:T(8,128)}), f32[16,104,128]{2,1,0:T(8,128)S(1)}, u32[]{:S(2)}, u32[]{:S(2)}) async-start(f32[16,104,128]{2,1,0:T(8,128)} %get-tuple-element.63), calls=%async_computation.5 | async-start | bytes 1703936 | tf_op jit(solution)/shard_map/all_to_all | solution.py:349
  124.3 5.7 %collective-permute-start.22 = (f32[2,64,128]{2,1,0:T(8,128)S(1)}, f32[2,64,128]{2,1,0:T(8,128)S(1)}, u32[]{:S(2)}, u32[]{:S(2)}) collective-permute-start(f32[2,64,128]{2,1,0:T(8,128)S(1)} %get-tuple-element.61.s0), channel_id=1, source_target_pairs={{0,4},{2,6},{4,0},{6,2},{8,12},{10,14},{12,8},{14,10},{1,5},{3,7},... | collective-permute-start | bytes 196616 | tf_op jit(solution)/shard_map/ppermute | solution.py:365
  125.9 7.7 %collective-permute-start.23 = (f32[2,64,128]{2,1,0:T(8,128)S(1)}, f32[2,64,128]{2,1,0:T(8,128)S(1)}, u32[]{:S(2)}, u32[]{:S(2)}) collective-permute-start(f32[2,64,128]{2,1,0:T(8,128)S(1)} %get-tuple-element.61.s0), channel_id=1, source_target_pairs={{0,8},{2,10},{4,12},{6,14},{8,0},{10,2},{12,4},{14,6},{1,9},{3,11}... | collective-permute-start | bytes 196616 | tf_op jit(solution)/shard_map/ppermute | solution.py:365
  128.3 6.5 %collective-permute-start.24 = (f32[2,64,128]{2,1,0:T(8,128)S(1)}, f32[2,64,128]{2,1,0:T(8,128)S(1)}, u32[]{:S(2)}, u32[]{:S(2)}) collective-permute-start(f32[2,64,128]{2,1,0:T(8,128)S(1)} %get-tuple-element.61.s0), channel_id=1, source_target_pairs={{0,12},{2,14},{4,8},{6,10},{8,4},{10,6},{12,0},{14,2},{1,13},{3,15... | collective-permute-start | bytes 196616 | tf_op jit(solution)/shard_map/ppermute | solution.py:365
  134.8 4.1 %collective-permute-start.25 = (f32[8,64,128]{2,1,0:T(8,128)S(1)}, f32[8,64,128]{2,1,0:T(8,128)S(1)}, u32[]{:S(2)}, u32[]{:S(2)}) collective-permute-start(f32[8,64,128]{2,1,0:T(8,128)S(1)} %shard_map.106.az), channel_id=1, source_target_pairs={{0,1},{1,0},{2,3},{3,2},{4,5},{5,4},{6,7},{7,6},{8,9},{9,8},{10,11... | collective-permute-start | bytes 786440 | tf_op jit(solution)/shard_map/ppermute | solution.py:353
  141.3 23.5 %all-to-all-start.6 = ((f32[256,1,128]{2,1,0:T(1,128)}), f32[256,1,128]{2,1,0:T(1,128)S(1)}, u32[]{:S(2)}, u32[]{:S(2)}) async-start(f32[256,1,128]{2,1,0:T(1,128)} %get-tuple-element.69), calls=%async_computation.6 | async-start | bytes 262144 | tf_op jit(solution)/shard_map/all_to_all | solution.py:434
